TPU v7x, 32 devices: a whole 2x2x4 slice. The times are simulated.
32 devices in a mesh: seq: 4 (over x, core), tp: 8 (over z, y).
Axes of the slice: x: 2, y: 2, z: 4, core: 2. Of those that a mesh axis runs over, the one named last changes fastest.
Arguments:
- vit_input: bfloat16 [2048, 1280], P(('seq', 'tp')), may hold values from -6 to 6
- image_lengths: int32 [4, 2], P('seq'), may hold values from 1 to 96, 128 in all within a row
- positions: int32 [512], replicated, may hold values from 0 to 511, each once
- vit_ln_gain: float32 [1280], replicated, may hold values from 0.25 to 1.75
- w_qkv: bfloat16 [1280, 3, 1280], P(None, None, 'tp'), may hold values from -0.15625 to 0.15625
- w_proj: bfloat16 [1280, 1280], P('tp'), may hold values from -0.15625 to 0.15625
- merger_ln_gain: float32 [1280], replicated, may hold values from 0.25 to 1.75
- merger_w1: bfloat16 [5120, 5120], P(None, 'tp'), may hold values from -0.078125 to 0.078125
- merger_w2: bfloat16 [5120, 8192], P('tp'), may hold values from -0.36336105 to 0.36336105
- norm_gain: float32 [8192], P('seq'), may hold values from 0.25 to 1.75
- gate_up_weight: bfloat16 [8192, 2, 29568], P('seq', None, 'tp'), may hold values from -0.0625 to 0.0625
- down_weight: bfloat16 [29568, 8192], P('tp', 'seq'), may hold values from -0.125 to 0.125
Outputs:
- mixed: bfloat16 [512, 8192], P('tp', 'seq')
Inputs may be any that keep to these rules, and one draw needn't show every extreme that they name: `image_lengths`: each row sums to 128. `positions`: a permutation: every slot once.
All inputs are finite; a program needn't handle non-finite values.
Results may differ from a plain program's by a relative error of at most 0.038.
Values may be sent and summed in bfloat16 or wider, within the bound.
A program may use at most 128 MiB of HBM per device.

v0:
```python
import functools

import jax
import jax.numpy as jnp
from jax import lax
from jax.experimental import pallas as pl
from jax.experimental.pallas import tpu as pltpu
from jax.sharding import PartitionSpec as P

D = 8192
HD = 80
MESH = pl.DeviceIdType.MESH
VM = pl.BlockSpec(memory_space=pltpu.VMEM)


def factors(n):
    minor = max(d for d in range(1, n + 1) if n % d == 0 and d * d <= n)
    return n // minor, minor


def greet(axis, peers):
    barrier = pltpu.get_barrier_semaphore()
    for peer in peers:
        pl.semaphore_signal(barrier, inc=1, device_id={axis: peer}, device_id_type=MESH)
    pl.semaphore_wait(barrier, len(peers))


def grid_peers(n_a, n_b, a, b):
    along_a = [lax.rem(a + da, n_a) * n_b + b for da in range(1, n_a)]
    along_b = [a * n_b + lax.rem(b + db, n_b) for db in range(1, n_b)]
    return along_a, along_b


def remote(src, dst, send_sem, recv_sem, axis, peer):
    return pltpu.make_async_remote_copy(
        src_ref=src,
        dst_ref=dst,
        send_sem=send_sem,
        recv_sem=recv_sem,
        device_id={axis: peer},
        device_id_type=MESH,
    )


def send(*args):
    copy = remote(*args)
    copy.start()
    return copy


def gather_kernel(axis, n, x_ref, out_ref, a_send, a_recv, b_send, b_recv, own_sem):
    n_a, n_b = factors(n)
    me = lax.axis_index(axis)
    a, b = me // n_b, lax.rem(me, n_b)
    along_a, along_b = grid_peers(n_a, n_b, a, b)
    greet(axis, along_a + along_b)
    a_copies, b_copies = [None], []
    for da in range(1, n_a):
        a_copies.append(
            send(x_ref, out_ref.at[me], a_send.at[da - 1], a_recv.at[da - 1], axis, along_a[da - 1])
        )
    own = pltpu.make_async_copy(x_ref, out_ref.at[me], own_sem)
    own.start()
    for db in range(1, n_b):
        b_copies.append(
            send(x_ref, out_ref.at[me], b_send.at[0, db - 1], b_recv.at[0, db - 1], axis, along_b[db - 1])
        )
    order = sorted(range(1, n_a), key=lambda da: min(da, n_a - da))
    for da in order:
        a_copies[da].wait_recv()
        source = lax.rem(a - da + n_a, n_a) * n_b + b
        for db in range(1, n_b):
            b_copies.append(
                send(
                    out_ref.at[source],
                    out_ref.at[source],
                    b_send.at[da, db - 1],
                    b_recv.at[da, db - 1],
                    axis,
                    along_b[db - 1],
                )
            )
    for copy in b_copies:
        copy.wait()
    for copy in a_copies[1:]:
        copy.wait_send()
    own.wait()


def gather(x, axis, collective_id):
    n = lax.axis_size(axis)
    n_a, n_b = factors(n)
    dma = pltpu.SemaphoreType.DMA
    return pl.pallas_call(
        functools.partial(gather_kernel, axis, n),
        out_shape=jax.ShapeDtypeStruct((n,) + x.shape, x.dtype),
        in_specs=[VM],
        out_specs=VM,
        scratch_shapes=[
            dma((n_a,)),
            dma((n_a,)),
            dma((n_a, n_b)),
            dma((n_a, n_b)),
            dma,
        ],
        name=f"gather{collective_id}",
        compiler_params=pltpu.CompilerParams(collective_id=collective_id, has_side_effects=True),
    )(x)


def scatter_kernel(axis, n, x_ref, out_ref, r1, y, r2, a_send, a_recv, b_send, b_recv):
    n_a, n_b = factors(n)
    me = lax.axis_index(axis)
    a, b = me // n_b, lax.rem(me, n_b)
    along_a, along_b = grid_peers(n_a, n_b, a, b)
    greet(axis, along_a + along_b)
    order = sorted(range(1, n_a), key=lambda da: -min(da, n_a - da)) + [0]
    b_copies, a_copies = {}, []
    for da in order:
        for db in range(1, n_b):
            block = lax.rem(a + da, n_a) * n_b + lax.rem(b + db, n_b)
            b_copies[da, db] = send(
                x_ref.at[block],
                r1.at[da, db - 1],
                b_send.at[da, db - 1],
                b_recv.at[da, db - 1],
                axis,
                along_b[db - 1],
            )

    def arrived(da):
        total = x_ref[lax.rem(a + da, n_a) * n_b + b].astype(jnp.float32)
        for db in range(1, n_b):
            b_copies[da, db].wait_recv()
            total = total + r1[da, db - 1].astype(jnp.float32)
        return total

    for da in order[:-1]:
        y[da - 1] = arrived(da).astype(y.dtype)
        a_copies.append(
            send(y.at[da - 1], r2.at[da - 1], a_send.at[da - 1], a_recv.at[da - 1], axis, along_a[da - 1])
        )
    total = arrived(0)
    for da, copy in zip(order[:-1], a_copies):
        copy.wait_recv()
        total = total + r2[da - 1].astype(jnp.float32)
    out_ref[...] = total.astype(out_ref.dtype)
    for copy in b_copies.values():
        copy.wait_send()
    for copy in a_copies:
        copy.wait_send()


def scatter_sum(x, axis, dtype, collective_id):
    n = lax.axis_size(axis)
    n_a, n_b = factors(n)
    block = x.shape[1:]
    dma = pltpu.SemaphoreType.DMA
    return pl.pallas_call(
        functools.partial(scatter_kernel, axis, n),
        out_shape=jax.ShapeDtypeStruct(block, dtype),
        in_specs=[VM],
        out_specs=VM,
        scratch_shapes=[
            pltpu.VMEM((n_a, n_b - 1) + block, x.dtype),
            pltpu.VMEM((n_a - 1,) + block, x.dtype),
            pltpu.VMEM((n_a - 1,) + block, x.dtype),
            dma((n_a,)),
            dma((n_a,)),
            dma((n_a, n_b)),
            dma((n_a, n_b)),
        ],
        name=f"scatter_sum{collective_id}",
        compiler_params=pltpu.CompilerParams(collective_id=collective_id, has_side_effects=True),
    )(x)


def exchange_kernel(axis, n, x_ref, out_ref, send_sem, recv_sem, own_sem):
    me = lax.axis_index(axis)
    peers = [lax.rem(me + d, n) for d in range(1, n)]
    greet(axis, peers)
    copies = [
        send(x_ref.at[peer], out_ref.at[me], send_sem.at[i], recv_sem.at[i], axis, peer)
        for i, peer in enumerate(peers)
    ]
    own = pltpu.make_async_copy(x_ref.at[me], out_ref.at[me], own_sem)
    own.start()
    for copy in copies:
        copy.wait()
    own.wait()


def exchange(x, axis, collective_id):
    n = lax.axis_size(axis)
    dma = pltpu.SemaphoreType.DMA
    return pl.pallas_call(
        functools.partial(exchange_kernel, axis, n),
        out_shape=jax.ShapeDtypeStruct(x.shape, x.dtype),
        in_specs=[VM],
        out_specs=VM,
        scratch_shapes=[dma((n,)), dma((n,)), dma],
        name=f"exchange{collective_id}",
        compiler_params=pltpu.CompilerParams(collective_id=collective_id, has_side_effects=True),
    )(x)


def hidden_kernel(axis, n, x_ref, w_ref, h_ref, held, gu_ref, w_sem, r1, y, r2, own_h, b_send, b_recv, a_send, a_recv, ga_send, ga_recv, gb_send, gb_recv, own_sem):
    n_a, n_b = factors(n)
    chunks = gu_ref.shape[0]
    width = gu_ref.shape[3] // n
    me = lax.axis_index(axis)
    a, b = me // n_b, lax.rem(me, n_b)
    along_a, along_b = grid_peers(n_a, n_b, a, b)

    def lanes(owner):
        return pl.ds(pl.multiple_of(owner * width, width), width)

    greet(axis, along_a + along_b)
    order = sorted(range(1, n_a), key=lambda da: -min(da, n_a - da)) + [0]
    b_copies, a_copies, ga, gb, local = {}, {}, {}, [], []

    def load(c):
        return pltpu.make_async_copy(w_ref.at[:, c], held.at[lax.rem(c, 2)], w_sem.at[lax.rem(c, 2)])

    def to_minor(c, da, db):
        block = lax.rem(a + da, n_a) * n_b + lax.rem(b + db, n_b)
        return remote(
            gu_ref.at[c, :, :, lanes(block)],
            r1.at[c, da, db - 1],
            b_send.at[c, da, db - 1],
            b_recv.at[c, da, db - 1],
            axis,
            along_b[db - 1],
        )

    def to_major(c, da):
        return remote(
            y.at[c, da - 1],
            r2.at[c, da - 1],
            a_send.at[c, da - 1],
            a_recv.at[c, da - 1],
            axis,
            along_a[da - 1],
        )

    def arrived(c, da):
        block = lax.rem(a + da, n_a) * n_b + b
        total = gu_ref[c, :, :, lanes(block)].astype(jnp.float32)
        for db in range(1, n_b):
            to_minor(c, da, db).wait_recv()
            total = total + r1[c, da, db - 1].astype(jnp.float32)
        return total

    def pass_on(c):
        for da in order[:-1]:
            y[c, da - 1] = arrived(c, da).astype(y.dtype)
            to_major(c, da).start()

    load(0).start()

    def product(c, carry):
        load(c).wait()

        @pl.when(c + 1 < chunks)
        def _():
            load(c + 1).start()

        for half in range(2):
            gu_ref[c, half] = lax.dot_general(
                held[lax.rem(c, 2), half],
                x_ref[...],
                (((1,), (1,)), ((), ())),
                preferred_element_type=jnp.float32,
            ).astype(gu_ref.dtype)
        for da in order:
            for db in range(1, n_b):
                to_minor(c, da, db).start()

        @pl.when(c > 0)
        def _():
            pass_on(c - 1)

        return carry

    lax.fori_loop(0, chunks, product, 0)
    pass_on(chunks - 1)
    for c in range(chunks):
        for da in order:
            for db in range(1, n_b):
                b_copies[c, da, db] = to_minor(c, da, db)
        for da in order[:-1]:
            a_copies[c, da] = to_major(c, da)

    def relay(c):
        for da in sorted(range(1, n_a), key=lambda da: min(da, n_a - da)):
            ga[c, da].wait_recv()
            source = h_ref.at[c, :, lanes(lax.rem(a - da + n_a, n_a) * n_b + b)]
            for db in range(1, n_b):
                gb.append(
                    send(source, source, gb_send.at[c, da, db - 1], gb_recv.at[c, da, db - 1], axis, along_b[db - 1])
                )

    for c in range(chunks):
        total = arrived(c, 0)
        for da in order[:-1]:
            a_copies[c, da].wait_recv()
            total = total + r2[c, da - 1].astype(jnp.float32)
        own_h[c] = (jax.nn.silu(total[0]) * total[1]).astype(own_h.dtype)
        target = h_ref.at[c, :, lanes(me)]
        for da in order[:-1]:
            ga[c, da] = send(own_h.at[c], target, ga_send.at[c, da - 1], ga_recv.at[c, da - 1], axis, along_a[da - 1])
        for db in range(1, n_b):
            gb.append(send(own_h.at[c], target, gb_send.at[c, 0, db - 1], gb_recv.at[c, 0, db - 1], axis, along_b[db - 1]))
        copy = pltpu.make_async_copy(own_h.at[c], target, own_sem.at[c])
        copy.start()
        local.append(copy)
    for c in range(chunks):
        relay(c)
    for copy in gb:
        copy.wait()
    for copy in list(b_copies.values()) + list(a_copies.values()) + list(ga.values()):
        copy.wait_send()
    for copy in local:
        copy.wait()


def hidden_values(x, weight, axis, collective_id):
    n = lax.axis_size(axis)
    n_a, n_b = factors(n)
    _, chunks, rows, depth = weight.shape
    tokens = x.shape[0]
    width = tokens // n
    dma = pltpu.SemaphoreType.DMA
    pair = (2, rows, width)
    return pl.pallas_call(
        functools.partial(hidden_kernel, axis, n),
        out_shape=jax.ShapeDtypeStruct((chunks, rows, tokens), x.dtype),
        in_specs=[VM, pl.BlockSpec(memory_space=pl.ANY)],
        out_specs=VM,
        scratch_shapes=[
            pltpu.VMEM((2, 2, rows, depth), x.dtype),
            pltpu.VMEM((chunks, 2, rows, tokens), x.dtype),
            dma((2,)),
            pltpu.VMEM((chunks, n_a, n_b - 1) + pair, x.dtype),
            pltpu.VMEM((chunks, n_a - 1) + pair, x.dtype),
            pltpu.VMEM((chunks, n_a - 1) + pair, x.dtype),
            pltpu.VMEM((chunks, rows, width), x.dtype),
            dma((chunks, n_a, n_b)),
            dma((chunks, n_a, n_b)),
            dma((chunks, n_a)),
            dma((chunks, n_a)),
            dma((chunks, n_a)),
            dma((chunks, n_a)),
            dma((chunks, n_a, n_b)),
            dma((chunks, n_a, n_b)),
            dma((chunks,)),
        ],
        name="hidden",
        compiler_params=pltpu.CompilerParams(
            collective_id=collective_id, has_side_effects=True, vmem_limit_bytes=67_000_000
        ),
    )(x, weight)


def chunk_count(rows):
    for count in (7, 6, 4, 3, 2):
        if rows % (count * 8) == 0:
            return count
    return 1


def layer_norm(values, gain):
    mean = jnp.mean(values, axis=-1, keepdims=True)
    centered = values - mean
    variance = jnp.mean(centered * centered, axis=-1, keepdims=True)
    return centered * lax.rsqrt(variance + 1e-06) * gain


def image_ids(lengths, count):
    image_ends = jnp.cumsum(lengths) * 4
    patch_index = jnp.arange(count, dtype=jnp.int32)
    return jnp.sum((patch_index[:, None] >= image_ends[None, :]).astype(jnp.int32), axis=1)


def attend(query, keys, values, image_index):
    scores = jnp.einsum("qhe,khe->hqk", query, keys, preferred_element_type=jnp.float32) * HD ** (
        -0.5
    )
    same_image = image_index[:, None] == image_index[None, :]
    scores = jnp.where(same_image[None], scores, -1e30)
    top = jnp.max(scores, axis=-1, keepdims=True)
    expo = jnp.exp(scores - top)
    weights = (expo / jnp.sum(expo, axis=-1, keepdims=True)).astype(jnp.bfloat16)
    output = jnp.einsum("hqk,khe->qhe", weights, values, preferred_element_type=jnp.float32)
    return output.astype(jnp.bfloat16)


def local(
    vit_input,
    image_lengths,
    positions,
    vit_ln_gain,
    w_qkv,
    w_proj,
    merger_ln_gain,
    merger_w1,
    merger_w2,
    norm_gain,
    gate_up_weight,
    down_weight,
):
    tp_size = lax.axis_size("tp")
    own_patches = vit_input.shape[0]
    patch_width = vit_input.shape[1]
    head_cols = w_qkv.shape[2]
    local_heads = head_cols // HD
    normed_patches = layer_norm(vit_input.astype(jnp.float32), vit_ln_gain).astype(jnp.bfloat16)
    w_qkv_flat = w_qkv.reshape(patch_width, 3 * head_cols)
    projected = jnp.dot(
        gather(normed_patches, "tp", 0).reshape(tp_size * own_patches, patch_width),
        w_qkv_flat,
        preferred_element_type=jnp.float32,
    ).astype(jnp.bfloat16)
    group_patches = projected.shape[0]
    projected = projected.reshape(group_patches, 3, local_heads, HD)
    image_index = image_ids(image_lengths[0], group_patches)
    attended = attend(projected[:, 0], projected[:, 1], projected[:, 2], image_index).reshape(
        group_patches, head_cols
    )
    attn_part = jnp.dot(attended, w_proj, preferred_element_type=jnp.float32).astype(jnp.bfloat16)
    attn_sum = scatter_sum(
        attn_part.reshape(tp_size, own_patches, patch_width), "tp", jnp.float32, 1
    )
    vit_out = vit_input.astype(jnp.float32) + attn_sum
    own_tokens = own_patches // 4
    merged_in = (
        layer_norm(vit_out, merger_ln_gain)
        .astype(jnp.bfloat16)
        .reshape(own_tokens, 4 * patch_width)
    )
    expanded = jax.nn.gelu(
        jnp.dot(
            gather(merged_in, "tp", 2).reshape(tp_size * own_tokens, 4 * patch_width),
            merger_w1,
            preferred_element_type=jnp.float32,
        ),
        approximate=False,
    ).astype(jnp.bfloat16)
    vis_part = jnp.dot(expanded, merger_w2, preferred_element_type=jnp.float32).astype(jnp.bfloat16)
    model_width = merger_w2.shape[1]
    vis_rows = scatter_sum(
        vis_part.reshape(tp_size, own_tokens, model_width), "tp", jnp.bfloat16, 3
    )
    seq_size = lax.axis_size("seq")
    slice_width = model_width // seq_size
    vis_values = vis_rows.astype(jnp.float32)
    row_squares = jnp.sum(vis_values * vis_values, axis=1, keepdims=True)
    inverse = lax.rsqrt(row_squares / D + 1e-06)
    high = inverse.astype(jnp.bfloat16).astype(jnp.float32)
    middle = (inverse - high).astype(jnp.bfloat16).astype(jnp.float32)
    lane = lax.broadcasted_iota(jnp.int32, (own_tokens, 128), 1)
    tail = jnp.where(
        lane == 0, high, jnp.where(lane == 1, middle, jnp.where(lane == 2, inverse - high - middle, 0.0))
    ).astype(jnp.bfloat16)
    payload = jnp.stack(
        [
            jnp.concatenate([vis_rows[:, s * slice_width : (s + 1) * slice_width], tail], axis=1)
            for s in range(seq_size)
        ]
    )
    own_slice = exchange(payload, "seq", 4)
    own_slice = own_slice.reshape(seq_size * own_tokens, slice_width + 128)
    seq_rows = tp_size * seq_size * own_tokens
    all_tokens = gather(own_slice, "tp", 5).reshape(seq_rows, slice_width + 128)
    slots = positions.reshape(seq_size, tp_size, own_tokens).transpose(1, 0, 2).reshape(seq_rows)
    row = lax.broadcasted_iota(jnp.int32, (seq_rows, seq_rows), 0)
    pick = (row == slots[None, :]).astype(jnp.bfloat16)
    ordered = jnp.dot(pick, all_tokens, preferred_element_type=jnp.float32)
    token_values = ordered[:, :slice_width]
    inverse_rms = jnp.sum(ordered[:, slice_width : slice_width + 3], axis=1, keepdims=True)
    normed = (token_values * inverse_rms * norm_gain).astype(jnp.bfloat16)
    hidden_width = gate_up_weight.shape[2]
    chunks = chunk_count(hidden_width)
    weight_rows = gate_up_weight.transpose(1, 2, 0).reshape(
        2, chunks, hidden_width // chunks, slice_width
    )
    hidden = hidden_values(normed, weight_rows, "seq", 6).reshape(hidden_width, seq_rows)
    terms = lax.dot_general(
        hidden, down_weight, (((0,), (0,)), ((), ())), preferred_element_type=jnp.float32
    ).astype(jnp.bfloat16)
    out_rows = seq_rows // tp_size
    down_sum = scatter_sum(terms.reshape(tp_size, out_rows, slice_width), "tp", jnp.float32, 7)
    residual = lax.dynamic_slice_in_dim(token_values, lax.axis_index("tp") * out_rows, out_rows, 0)
    return (residual + down_sum).astype(jnp.bfloat16)


def solution(mesh):
    return jax.shard_map(
        local,
        mesh=mesh,
        in_specs=(
            P(("seq", "tp"), None),
            P("seq", None),
            P(),
            P(),
            P(None, None, "tp"),
            P("tp", None),
            P(),
            P(None, "tp"),
            P("tp", None),
            P("seq"),
            P("seq", None, "tp"),
            P("tp", "seq"),
        ),
        out_specs=P("tp", "seq"),
        check_vma=False,
    )
```

profile of v0, /device:TPU:0, one launch (start us, length us, event | category | flops | bytes accessed | tf_op | source)
XLA Modules:
  0.0 325.6 jit_solution(15788898080263123602)
XLA Ops:
  0.0 1.1 convert_reduce_fusion
  1.2 1.1 fusion.9
  2.3 1.7 fusion.11.x_ref
  4.0 25.7 %gather0.1 = bf16[8,64,1280]{2,1,0:T(8,128)(2,1)} custom-call(bf16[64,1280]{1,0:T(8,128)(2,1)} %fusion.11.x_ref), custom_call_target="tpu_custom_call" | custom-call | tf_op jit(solution)/shard_map/gather0/pallas_call | solution.py:94
  29.7 2.1 convolution_convert_fusion.3
  32.4 1.0 fusion.103
  33.3 1.3 convolution_convert_fusion.4
  34.6 1.6 convolution_convert_fusion.1
  36.2 27.2 %scatter_sum1.1 = f32[64,1280]{1,0:T(8,128)} custom-call(bf16[8,64,1280]{2,1,0:T(8,128)(2,1)} %bitcast.67), custom_call_target="tpu_custom_call" | custom-call | tf_op jit(solution)/shard_map/scatter_sum1/pallas_call | solution.py:159
  63.4 1.1 fusion.56
  64.5 1.2 multiply_reduce_fusion.1
  65.8 1.1 multiply_convert_fusion.1
  67.6 21.8 %gather2.1 = bf16[8,16,5120]{2,1,0:T(8,128)(2,1)} custom-call(bf16[16,5120]{1,0:T(8,128)(2,1)} %reshape.158.x_ref), custom_call_target="tpu_custom_call" | custom-call | tf_op jit(solution)/shard_map/gather2/pallas_call | solution.py:94
  89.5 11.2 %convolution_convert_fusion = bf16[128,8192]{1,0:T(8,128)(2,1)} fusion(bf16[640,8192]{1,0:T(8,128)(2,1)} %param.20, bf16[128,5120]{1,0:T(8,128)(2,1)} %bitcast.72, bf16[5120,640]{1,0:T(8,128)(2,1)} %param.19), kind=kOutput, calls=%fused_computation.1 | convolution fusion | flops 2187411456 | bytes 20447232 | tf_op jit(solution)/shard_map/dot_general | solution.py:449
  100.7 36.2 %scatter_sum3.1 = bf16[16,8192]{1,0:T(8,128)(2,1)} custom-call(bf16[8,16,8192]{2,1,0:T(8,128)(2,1)} %bitcast.70), custom_call_target="tpu_custom_call" | custom-call | tf_op jit(solution)/shard_map/scatter_sum3/pallas_call | solution.py:159
  136.9 1.1 multiply_reduce_fusion
  139.9 6.8 %exchange4.1 = bf16[4,16,2176]{2,1,0:T(8,128)(2,1)} custom-call(bf16[4,16,2176]{2,1,0:T(8,128)(2,1)} %pad_maximum_fusion.x_ref), custom_call_target="tpu_custom_call" | custom-call | tf_op jit(solution)/shard_map/exchange4/pallas_call | solution.py:196
  146.7 33.4 %gather5.1 = bf16[8,64,2176]{2,1,0:T(8,128)(2,1)} custom-call(bf16[64,2176]{1,0:T(8,128)(2,1)} %bitcast.73), custom_call_target="tpu_custom_call" | custom-call | tf_op jit(solution)/shard_map/gather5/pallas_call | solution.py:94
  180.3 3.0 fusion.4
  183.5 3.3 fusion.101
  186.8 77.0 %hidden.1 = bf16[7,528,512]{2,1,0:T(8,128)(2,1)} custom-call(bf16[512,2048]{1,0:T(8,128)(2,1)} %get-tuple-element.6.x_ref, bf16[2,7,528,2048]{3,2,1,0:T(8,128)(2,1)} %bitcast.65), custom_call_target="tpu_custom_call" | custom-call | tf_op jit(solution)/shard_map/hidden/pallas_call | solution.py:335
  263.7 13.8 %convolution_convert_fusion.2 = bf16[512,2048]{1,0:T(8,128)(2,1)} fusion(bf16[3696,512]{1,0:T(8,128)(2,1)} %bitcast.68, bf16[3696,2048]{1,0:T(8,128)(2,1)} %param.23), kind=kOutput, calls=%fused_computation.4 | convolution fusion | flops 7752122368 | bytes 21020672 | tf_op jit(solution)/shard_map/dot_general | solution.py:488
  277.5 46.1 %scatter_sum7.1 = f32[64,2048]{1,0:T(8,128)} custom-call(bf16[8,64,2048]{2,1,0:T(8,128)(2,1)} %bitcast.69), custom_call_target="tpu_custom_call" | custom-call | tf_op jit(solution)/shard_map/scatter_sum7/pallas_call | solution.py:159
  323.6 2.0 add_convert_fusion
  (35 shorter events, 3.5 us)
Async XLA Ops:
  0.0 29.7 %copy-start.5 = (bf16[1280,3,160]{0,2,1:T(8,128)(2,1)S(1)}, bf16[1280,3,160]{0,2,1:T(8,128)(2,1)}, u32[]{:S(2)}) copy-start(bf16[1280,3,160]{0,2,1:T(8,128)(2,1)} %param.16) | copy-start | bytes 3686404
  29.7 2.2 copy-start.6
  33.3 1.3 copy-start.1
  34.6 28.8 %copy-start = (bf16[64,1280]{1,0:T(8,128)(2,1)S(1)}, bf16[64,1280]{1,0:T(8,128)(2,1)}, u32[]{:S(2)}) copy-start(bf16[64,1280]{1,0:T(8,128)(2,1)} %param.12) | copy-start | bytes 491524
  34.6 31.1 %copy-start.3 = (f32[1280]{0:T(1024)S(1)}, f32[1280]{0:T(1024)}, u32[]{:S(2)}) copy-start(f32[1280]{0:T(1024)} %param.18) | copy-start | bytes 15364
  139.1 41.0 %copy-start.4 = (s32[512]{0:T(512)S(1)}, s32[512]{0:T(512)}, u32[]{:S(2)}) copy-start(s32[512]{0:T(512)} %param.14) | copy-start | bytes 6148
  180.3 3.2 copy-start.2
where the time goes:
time: 326 us
  Pallas kernels  274 us (84%)
  matrix products  34 us (10%)
  other arithmetic  15.2 us (5%)
    pallas_call x3, Pallas kernels, scatter_sum(): pl.pallas_call(functools.partial(scatter_kernel, axis, n), out_shape=jax....  109 us
    pallas_call x3, Pallas kernels, gather(): pl.pallas_call(functools.partial(gather_kernel, axis, n), out_shape=jax.S...  80.9 us
    pallas_call x1, Pallas kernels, hidden_values(): pl.pallas_call(functools.partial(hidden_kernel, axis, n), out_shape=jax.S...  77 us
    dot_general x1, matrix products, local(): lax.dot_general(hidden, down_weight, (((0,), (0,)), ((), ())), preferred_...  13.8 us
    dot_general x1, matrix products, local(): jnp.dot(expanded, merger_w2, preferred_element_type=jnp.float32)  11.2 us
    pallas_call x1, Pallas kernels, exchange(): pl.pallas_call(functools.partial(exchange_kernel, axis, n), out_shape=jax...  6.8 us

commit v1 on v0

v1 whole, which is shorter than its diff:
```python
import functools

import jax
import jax.numpy as jnp
from jax import lax
from jax.experimental import pallas as pl
from jax.experimental.pallas import tpu as pltpu
from jax.sharding import PartitionSpec as P

HD = 80
MESH = pl.DeviceIdType.MESH
VM = pl.BlockSpec(memory_space=pltpu.VMEM)


def factors(n):
    minor = max(d for d in range(1, n + 1) if n % d == 0 and d * d <= n)
    return n // minor, minor


def greet(axis, peers):
    barrier = pltpu.get_barrier_semaphore()
    for peer in peers:
        pl.semaphore_signal(barrier, inc=1, device_id={axis: peer}, device_id_type=MESH)
    pl.semaphore_wait(barrier, len(peers))


def grid_peers(n_a, n_b, a, b):
    along_a = [lax.rem(a + da, n_a) * n_b + b for da in range(1, n_a)]
    along_b = [a * n_b + lax.rem(b + db, n_b) for db in range(1, n_b)]
    return along_a, along_b


def remote(src, dst, send_sem, recv_sem, axis, peer):
    return pltpu.make_async_remote_copy(
        src_ref=src,
        dst_ref=dst,
        send_sem=send_sem,
        recv_sem=recv_sem,
        device_id={axis: peer},
        device_id_type=MESH,
    )


def send(*args):
    copy = remote(*args)
    copy.start()
    return copy


def gather_kernel(axis, n, x_ref, out_ref, a_send, a_recv, b_send, b_recv, own_sem):
    n_a, n_b = factors(n)
    me = lax.axis_index(axis)
    a, b = me // n_b, lax.rem(me, n_b)
    along_a, along_b = grid_peers(n_a, n_b, a, b)
    greet(axis, along_a + along_b)
    a_copies, b_copies = [None], []
    for da in range(1, n_a):
        a_copies.append(
            send(x_ref, out_ref.at[me], a_send.at[da - 1], a_recv.at[da - 1], axis, along_a[da - 1])
        )
    own = pltpu.make_async_copy(x_ref, out_ref.at[me], own_sem)
    own.start()
    for db in range(1, n_b):
        b_copies.append(
            send(x_ref, out_ref.at[me], b_send.at[0, db - 1], b_recv.at[0, db - 1], axis, along_b[db - 1])
        )
    order = sorted(range(1, n_a), key=lambda da: min(da, n_a - da))
    for da in order:
        a_copies[da].wait_recv()
        source = lax.rem(a - da + n_a, n_a) * n_b + b
        for db in range(1, n_b):
            b_copies.append(
                send(
                    out_ref.at[source],
                    out_ref.at[source],
                    b_send.at[da, db - 1],
                    b_recv.at[da, db - 1],
                    axis,
                    along_b[db - 1],
                )
            )
    for copy in b_copies:
        copy.wait()
    for copy in a_copies[1:]:
        copy.wait_send()
    own.wait()


def gather(x, axis, collective_id):
    n = lax.axis_size(axis)
    n_a, n_b = factors(n)
    dma = pltpu.SemaphoreType.DMA
    return pl.pallas_call(
        functools.partial(gather_kernel, axis, n),
        out_shape=jax.ShapeDtypeStruct((n,) + x.shape, x.dtype),
        in_specs=[VM],
        out_specs=VM,
        scratch_shapes=[
            dma((n_a,)),
            dma((n_a,)),
            dma((n_a, n_b)),
            dma((n_a, n_b)),
            dma,
        ],
        name=f"gather{collective_id}",
        compiler_params=pltpu.CompilerParams(collective_id=collective_id, has_side_effects=True),
    )(x)


def scatter_kernel(axis, n, x_ref, out_ref, r1, y, r2, a_send, a_recv, b_send, b_recv):
    n_a, n_b = factors(n)
    me = lax.axis_index(axis)
    a, b = me // n_b, lax.rem(me, n_b)
    along_a, along_b = grid_peers(n_a, n_b, a, b)
    greet(axis, along_a + along_b)
    order = sorted(range(1, n_a), key=lambda da: -min(da, n_a - da)) + [0]
    b_copies, a_copies = {}, []
    for da in order:
        for db in range(1, n_b):
            block = lax.rem(a + da, n_a) * n_b + lax.rem(b + db, n_b)
            b_copies[da, db] = send(
                x_ref.at[block],
                r1.at[da, db - 1],
                b_send.at[da, db - 1],
                b_recv.at[da, db - 1],
                axis,
                along_b[db - 1],
            )

    def arrived(da):
        total = x_ref[lax.rem(a + da, n_a) * n_b + b].astype(jnp.float32)
        for db in range(1, n_b):
            b_copies[da, db].wait_recv()
            total = total + r1[da, db - 1].astype(jnp.float32)
        return total

    for da in order[:-1]:
        y[da - 1] = arrived(da).astype(y.dtype)
        a_copies.append(
            send(y.at[da - 1], r2.at[da - 1], a_send.at[da - 1], a_recv.at[da - 1], axis, along_a[da - 1])
        )
    total = arrived(0)
    for da, copy in zip(order[:-1], a_copies):
        copy.wait_recv()
        total = total + r2[da - 1].astype(jnp.float32)
    out_ref[...] = total.astype(out_ref.dtype)
    for copy in b_copies.values():
        copy.wait_send()
    for copy in a_copies:
        copy.wait_send()


def scatter_sum(x, axis, dtype, collective_id):
    n = lax.axis_size(axis)
    n_a, n_b = factors(n)
    block = x.shape[1:]
    dma = pltpu.SemaphoreType.DMA
    return pl.pallas_call(
        functools.partial(scatter_kernel, axis, n),
        out_shape=jax.ShapeDtypeStruct(block, dtype),
        in_specs=[VM],
        out_specs=VM,
        scratch_shapes=[
            pltpu.VMEM((n_a, n_b - 1) + block, x.dtype),
            pltpu.VMEM((n_a - 1,) + block, x.dtype),
            pltpu.VMEM((n_a - 1,) + block, x.dtype),
            dma((n_a,)),
            dma((n_a,)),
            dma((n_a, n_b)),
            dma((n_a, n_b)),
        ],
        name=f"scatter_sum{collective_id}",
        compiler_params=pltpu.CompilerParams(collective_id=collective_id, has_side_effects=True),
    )(x)


SEMS = (
    "w2", "w", "d", "ea_s", "ea_r", "eb_s", "eb_r", "q_s", "q_r", "p_s", "p_r", "y_s", "y_r", "h_s", "h_r",
    "o_s", "b_r", "rb_s", "rb_r", "ra_s", "ra_r", "ga_s", "ga_r", "gb_s", "gb_r",
)
BUFS = (
    "ex", "w2s", "part", "r1", "yb", "r2", "tok", "nrm", "sqa", "rq", "inv", "held", "dheld", "gu", "pin",
    "keep", "yx", "rx", "hid", "acc",
)


def decoder_kernel(parts, e_ref, pos_ref, gain_ref, w2_ref, w_ref, d_ref, out_ref, *scratch):
    buf = dict(zip(BUFS, scratch))
    sem = dict(zip(SEMS, scratch[len(BUFS):]))
    n, m = lax.axis_size("seq"), lax.axis_size("tp")
    (n_a, n_b), (m_a, m_b) = factors(n), factors(m)
    me, mt = lax.axis_index("seq"), lax.axis_index("tp")
    a, b = me // n_b, lax.rem(me, n_b)
    ta, tb = mt // m_b, lax.rem(mt, m_b)
    x_peers, core_peers = grid_peers(n_a, n_b, a, b)
    t_major, t_minor = grid_peers(m_a, m_b, ta, tb)
    partner = core_peers[0]
    chunks, rows, depth = w_ref.shape[1:]
    steps = parts * chunks
    owned = steps // n_b
    count = n_a * 128
    block = count // m

    def to(axis, src, dst, s, r, peer):
        return remote(src, dst, s, r, axis, peer)

    def lanes(owner):
        return pl.ds(pl.multiple_of(owner * 128, 128), 128)

    w2_load = pltpu.make_async_copy(
        w2_ref.at[:, pl.ds(pl.multiple_of(me * depth, depth), depth)], buf["w2s"], sem["w2"]
    )

    def w_load(i):
        slot = lax.rem(i, 2)
        return pltpu.make_async_copy(w_ref.at[:, lax.rem(i, chunks)], buf["held"].at[slot], sem["w"].at[slot])

    def d_load(i):
        slot = lax.rem(i, 2)
        return pltpu.make_async_copy(d_ref.at[lax.rem(i, chunks)], buf["dheld"].at[slot], sem["d"].at[slot])

    w2_load.start()
    w_load(0).start()

    barrier = pltpu.get_barrier_semaphore()
    everyone = [("seq", lax.rem(me + d, n)) for d in range(1, n)]
    everyone += [("tp", peer) for peer in t_major + t_minor]
    for axis, peer in everyone:
        pl.semaphore_signal(barrier, inc=1, device_id={axis: peer}, device_id_type=MESH)
    pl.semaphore_wait(barrier, len(everyone))

    ex = buf["ex"]
    e_a = [
        to("seq", e_ref, ex.at[me], sem["ea_s"].at[da - 1], sem["ea_r"].at[da - 1], x_peers[da - 1])
        for da in range(1, n_a)
    ]
    e_b = [to("seq", e_ref, ex.at[me], sem["eb_s"].at[0], sem["eb_r"].at[0], partner)]
    for copy in e_a + e_b:
        copy.start()
    ex[me] = e_ref[...]
    for da in range(1, n_a):
        e_a[da - 1].wait_recv()
        source = ex.at[lax.rem(a - da + n_a, n_a) * n_b + b]
        copy = to("seq", source, source, sem["eb_s"].at[da], sem["eb_r"].at[da], partner)
        copy.start()
        e_b.append(copy)
    for copy in e_b:
        copy.wait()
    for copy in e_a:
        copy.wait_send()

    part, r1, yb, r2 = buf["part"], buf["r1"], buf["yb"], buf["r2"]
    order = sorted(range(1, m_a), key=lambda da: -min(da, m_a - da)) + [0]

    def rs_minor(u, da, db):
        at = lax.rem(ta + da, m_a) * m_b + lax.rem(tb + db, m_b)
        return to(
            "tp", part.at[u, at], r1.at[u, da, db - 1], sem["rb_s"].at[u, da, db - 1],
            sem["rb_r"].at[u, da, db - 1], t_minor[db - 1],
        )

    def rs_major(u, da):
        return to(
            "tp", yb.at[u, da - 1], r2.at[u, da - 1], sem["ra_s"].at[u, da - 1], sem["ra_r"].at[u, da - 1],
            t_major[da - 1],
        )

    def rs_start(u):
        for da in order:
            for db in range(1, m_b):
                rs_minor(u, da, db).start()

    def rs_arrived(u, da):
        total = part[u, lax.rem(ta + da, m_a) * m_b + tb].astype(jnp.float32)
        for db in range(1, m_b):
            rs_minor(u, da, db).wait_recv()
            total = total + r1[u, da, db - 1].astype(jnp.float32)
        return total

    def rs_pass(u):
        for da in order[:-1]:
            yb[u, da - 1] = rs_arrived(u, da).astype(yb.dtype)
            rs_major(u, da).start()

    def rs_finish(u):
        total = rs_arrived(u, 0)
        for da in order[:-1]:
            rs_major(u, da).wait_recv()
            total = total + r2[u, da - 1].astype(jnp.float32)
        for da in order:
            for db in range(1, m_b):
                rs_minor(u, da, db).wait_send()
        for da in order[:-1]:
            rs_major(u, da).wait_send()
        return total

    tok = buf["tok"]

    def ag_major(h, da):
        return to(
            "tp", tok.at[h, mt], tok.at[h, mt], sem["ga_s"].at[h, da - 1], sem["ga_r"].at[h, da - 1], t_major[da - 1]
        )

    def ag_minor(h, da, db):
        at = lax.rem(ta - da + m_a, m_a) * m_b + tb
        return to(
            "tp", tok.at[h, at], tok.at[h, at], sem["gb_s"].at[h, da, db - 1], sem["gb_r"].at[h, da, db - 1],
            t_minor[db - 1],
        )

    near = order[:-1][::-1]

    def ag_start(h):
        tok[h, mt] = rs_finish(h).astype(tok.dtype)
        for da in order[:-1]:
            ag_major(h, da).start()
        for db in range(1, m_b):
            ag_minor(h, 0, db).start()

    def ag_relay(h):
        for da in near:
            ag_major(h, da).wait_recv()
            for db in range(1, m_b):
                ag_minor(h, da, db).start()

    rq, inv, sqa, nrm = buf["rq"], buf["inv"], buf["sqa"], buf["nrm"]

    def squares(h, d):
        return to(
            "seq", rq.at[h, me], rq.at[h, me], sem["q_s"].at[h, d - 1], sem["q_r"].at[h, d - 1], lax.rem(me + d, n)
        )

    def ag_finish(h):
        for da in [0] + near:
            for db in range(1, m_b):
                ag_minor(h, da, db).wait()
        for da in near:
            ag_major(h, da).wait_send()

        def rows_of(t, carry):
            values = tok[h, t].astype(jnp.float32)
            at = pl.ds(pl.multiple_of(t * block, block), block)
            nrm[at] = (values * gain_ref[...]).astype(nrm.dtype)
            total = values[:, :128] * values[:, :128]
            for k in range(1, depth // 128):
                piece = values[:, k * 128 : (k + 1) * 128]
                total = total + piece * piece
            sqa[at] = total
            return carry

        lax.fori_loop(0, m, rows_of, 0)
        sums = jnp.sum(jnp.transpose(sqa[...]), axis=0, keepdims=True)
        rq[h, me] = jnp.broadcast_to(sums, (8, count))
        for d in range(1, n):
            squares(h, d).start()

    def inverse(h):
        for d in range(1, n):
            squares(h, d).wait()
        total = rq[h, 0]
        for s in range(1, n):
            total = total + rq[h, s]
        inv[h] = lax.rsqrt(total / (depth * n) + 1e-06)

    w2_load.wait()
    for h in range(parts):
        row = lax.broadcasted_iota(jnp.int32, (count, pos_ref.shape[1]), 0)
        slot = lax.shift_right_logical(row, block.bit_length() - 1) * (block * (parts - 1)) + row + h * block
        pick = (slot == pos_ref[...]).astype(jnp.bfloat16)
        moved = jnp.dot(
            pick, ex[...].reshape(pos_ref.shape[1], ex.shape[2]), preferred_element_type=jnp.float32
        ).astype(jnp.bfloat16)
        width = min(512, depth)
        for k in range(depth // width):
            piece = jnp.dot(
                moved, buf["w2s"][:, k * width : (k + 1) * width], preferred_element_type=jnp.float32
            ).astype(part.dtype)
            part[h, :, :, k * width : (k + 1) * width] = piece.reshape(m, block, width)
        if h == 0:
            rs_start(0)
    rs_pass(0)
    ag_start(0)
    ag_relay(0)
    ag_finish(0)

    gu, pin, keep, yx, rx, hid, acc = (buf[k] for k in ("gu", "pin", "keep", "yx", "rx", "hid", "acc"))

    def owner(i):
        return lax.rem(i, n_b) == b

    def to_owner(i):
        return to("seq", gu.at[lax.rem(i, 2)], pin.at[i // n_b], sem["p_s"].at[i // n_b], sem["p_r"].at[i // n_b], partner)

    def to_x(i, da):
        o = i // n_b
        return to(
            "seq", yx.at[o, da - 1], rx.at[o, da - 1], sem["y_s"].at[o, da - 1], sem["y_r"].at[o, da - 1], x_peers[da - 1]
        )

    def hid_x(i, da):
        target = hid.at[i, :, lanes(a)]
        return to("seq", target, target, sem["h_s"].at[i, da - 1], sem["h_r"].at[i, da - 1], x_peers[da - 1])

    def hid_core(i, da):
        target = hid.at[i, :, lanes(lax.rem(a - da + n_a, n_a))]
        return to("seq", target, target, sem["o_s"].at[i, da], sem["b_r"].at[i, da], partner)

    def stage_a(i):
        w_load(i).wait()

        @pl.when(i + 1 < steps)
        def _():
            w_load(i + 1).start()

        for half in range(2):
            gu[lax.rem(i, 2), half] = lax.dot_general(
                buf["held"][lax.rem(i, 2), half],
                nrm[...],
                (((1,), (1,)), ((), ())),
                preferred_element_type=jnp.float32,
            ).astype(gu.dtype)

        @pl.when(jnp.logical_not(owner(i)))
        def _():
            to_owner(i).start()

    def stage_b(i):
        o = i // n_b

        @pl.when(owner(i))
        def _():
            to_owner(i).wait_recv()

            def both(da):
                at = lanes(lax.rem(a + da, n_a))
                return gu[lax.rem(i, 2), :, :, at].astype(jnp.float32) + pin[o, :, :, at].astype(jnp.float32)

            for da in range(1, n_a):
                yx[o, da - 1] = both(da).astype(yx.dtype)
                to_x(i, da).start()
            keep[lax.rem(o, 2)] = both(0)

        @pl.when(jnp.logical_not(owner(i)))
        def _():
            to_owner(i).wait_send()

    def stage_c(i):
        o, h = i // n_b, i // chunks

        @pl.when(lax.rem(i, chunks) == 0)
        def _():
            inverse(h)

        @pl.when(owner(i))
        def _():
            total = keep[lax.rem(o, 2)]
            for da in range(1, n_a):
                to_x(i, da).wait()
                total = total + rx[o, da - 1].astype(jnp.float32)
            total = total * inv[h, 0:1, lanes(a)]
            hid[i, :, lanes(a)] = (jax.nn.silu(total[0]) * total[1]).astype(hid.dtype)
            for da in range(1, n_a):
                hid_x(i, da).start()
            hid_core(i, 0).start()

    def stage_d(i):
        @pl.when(owner(i))
        def _():
            for da in range(1, n_a):
                hid_x(i, da).wait()
                hid_core(i, da).start()

    def stage_e(i):
        c, h = lax.rem(i, chunks), i // chunks

        @pl.when(owner(i))
        def _():
            for da in range(n_a):
                hid_core(i, da).wait_send()

        @pl.when(jnp.logical_not(owner(i)))
        def _():
            for da in range(n_a):
                hid_core(i, da).wait_recv()

        d_load(i).wait()
        width = min(512, depth)
        left = hid[i]
        for k in range(depth // width):
            at = slice(k * width, (k + 1) * width)
            piece = lax.dot_general(
                left, buf["dheld"][lax.rem(i, 2), :, at], (((0,), (0,)), ((), ())), preferred_element_type=jnp.float32
            )

            @pl.when(c == 0)
            def _():
                acc[:, at] = piece

            @pl.when(c > 0)
            def _():
                acc[:, at] += piece

        @pl.when(c == chunks - 1)
        def _():
            part[parts + h] = acc[...].astype(part.dtype).reshape(m, block, depth)
            rs_start(parts + h)

    def output(h):
        at = pl.ds(pl.multiple_of(h * block, block), block)
        total = rs_finish(parts + h)
        out_ref[at] = (tok[h, mt].astype(jnp.float32) + total).astype(out_ref.dtype)

    k_pass, k_gather, k_relay = 2 * chunks // 7, 4 * chunks // 7, 6 * chunks // 7

    def iteration(i, carry):
        def when(lag, fn):
            @pl.when(jnp.logical_and(i >= lag, i - lag < steps))
            def _():
                fn(i - lag)

        h, k = i // chunks, lax.rem(i, chunks)
        more = h + 1 < parts

        def at_step(step, fn):
            @pl.when(jnp.logical_and(more, k == step))
            def _():
                fn(h + 1)

        @pl.when(jnp.logical_and(jnp.logical_and(i > 0, i < steps), k == 0))
        def _():
            ag_finish(h)

        at_step(0, rs_start)
        when(3, lambda j: d_load(j).start())
        when(0, stage_a)
        when(1, stage_b)
        when(2, stage_c)
        when(3, stage_d)
        at_step(k_pass, rs_pass)
        at_step(k_gather, ag_start)
        at_step(k_relay, ag_relay)
        when(4, stage_e)

        def later(lag, fn):
            @pl.when(jnp.logical_and(i - lag >= chunks, jnp.logical_and(lax.rem(i - lag + chunks, chunks) == 0, i - lag < steps)))
            def _():
                fn((i - lag) // chunks - 1)

        later(5, lambda h: rs_pass(parts + h))
        later(7, output)
        return carry

    lax.fori_loop(0, steps + 4, iteration, 0)
    rs_pass(2 * parts - 1)
    output(parts - 1)


def decoder(expanded, positions, gain, w2, weight, down, collective_id):
    n, m = lax.axis_size("seq"), lax.axis_size("tp")
    (n_a, n_b), (m_a, m_b) = factors(n), factors(m)
    _, chunks, rows, depth = weight.shape
    tokens = positions.shape[1]
    count = n_a * 128
    parts = tokens // count
    steps = parts * chunks
    block = count // m
    assert n_b == 2 and steps % 2 == 0 and chunks >= 7
    kind, f32 = expanded.dtype, jnp.float32
    shapes = {
        "ex": ((n,) + expanded.shape, kind),
        "w2s": ((w2.shape[0], depth), kind),
        "part": ((2 * parts, m, block, depth), kind),
        "r1": ((2 * parts, m_a, m_b - 1, block, depth), kind),
        "yb": ((2 * parts, m_a - 1, block, depth), kind),
        "r2": ((2 * parts, m_a - 1, block, depth), kind),
        "tok": ((parts, m, block, depth), kind),
        "nrm": ((count, depth), kind),
        "sqa": ((count, 128), f32),
        "rq": ((parts, n, 8, count), f32),
        "inv": ((parts, 8, count), f32),
        "held": ((2, 2, rows, depth), kind),
        "dheld": ((2, rows, depth), kind),
        "gu": ((2, 2, rows, count), kind),
        "pin": ((steps // 2, 2, rows, count), kind),
        "keep": ((2, 2, rows, 128), f32),
        "yx": ((steps // 2, n_a - 1, 2, rows, 128), kind),
        "rx": ((steps // 2, n_a - 1, 2, rows, 128), kind),
        "hid": ((steps, rows, count), kind),
        "acc": ((count, depth), f32),
    }
    sems = {
        "w2": (),
        "w": (2,),
        "d": (2,),
        "ea_s": (n_a,),
        "ea_r": (n_a,),
        "eb_s": (n_a,),
        "eb_r": (n_a,),
        "q_s": (parts, n),
        "q_r": (parts, n),
        "p_s": (steps // 2,),
        "p_r": (steps // 2,),
        "y_s": (steps // 2, n_a),
        "y_r": (steps // 2, n_a),
        "h_s": (steps, n_a),
        "h_r": (steps, n_a),
        "o_s": (steps, n_a),
        "b_r": (steps, n_a),
        "rb_s": (2 * parts, m_a, m_b),
        "rb_r": (2 * parts, m_a, m_b),
        "ra_s": (2 * parts, m_a),
        "ra_r": (2 * parts, m_a),
        "ga_s": (parts, m_a),
        "ga_r": (parts, m_a),
        "gb_s": (parts, m_a, m_b),
        "gb_r": (parts, m_a, m_b),
    }
    anywhere = pl.BlockSpec(memory_space=pl.ANY)
    return pl.pallas_call(
        functools.partial(decoder_kernel, parts),
        out_shape=jax.ShapeDtypeStruct((tokens // m, depth), kind),
        in_specs=[VM, VM, VM, anywhere, anywhere, anywhere],
        out_specs=VM,
        scratch_shapes=[pltpu.VMEM(*shapes[k]) for k in BUFS]
        + [pltpu.SemaphoreType.DMA(sems[k]) if sems[k] else pltpu.SemaphoreType.DMA for k in SEMS],
        name="decoder",
        compiler_params=pltpu.CompilerParams(
            collective_id=collective_id, has_side_effects=True, vmem_limit_bytes=67_000_000
        ),
    )(expanded, positions, gain, w2, weight, down)


def chunk_count(rows):
    for count in (7, 6, 4, 3, 2):
        if rows % (count * 8) == 0:
            return count
    return 1


def layer_norm(values, gain):
    mean = jnp.mean(values, axis=-1, keepdims=True)
    centered = values - mean
    variance = jnp.mean(centered * centered, axis=-1, keepdims=True)
    return centered * lax.rsqrt(variance + 1e-06) * gain


def image_ids(lengths, count):
    image_ends = jnp.cumsum(lengths) * 4
    patch_index = jnp.arange(count, dtype=jnp.int32)
    return jnp.sum((patch_index[:, None] >= image_ends[None, :]).astype(jnp.int32), axis=1)


def attend(query, keys, values, image_index):
    scores = jnp.einsum("qhe,khe->hqk", query, keys, preferred_element_type=jnp.float32) * HD ** (
        -0.5
    )
    same_image = image_index[:, None] == image_index[None, :]
    scores = jnp.where(same_image[None], scores, -1e30)
    top = jnp.max(scores, axis=-1, keepdims=True)
    expo = jnp.exp(scores - top)
    weights = (expo / jnp.sum(expo, axis=-1, keepdims=True)).astype(jnp.bfloat16)
    output = jnp.einsum("hqk,khe->qhe", weights, values, preferred_element_type=jnp.float32)
    return output.astype(jnp.bfloat16)


def local(
    vit_input,
    image_lengths,
    positions,
    vit_ln_gain,
    w_qkv,
    w_proj,
    merger_ln_gain,
    merger_w1,
    merger_w2,
    norm_gain,
    gate_up_weight,
    down_weight,
):
    tp_size = lax.axis_size("tp")
    own_patches = vit_input.shape[0]
    patch_width = vit_input.shape[1]
    head_cols = w_qkv.shape[2]
    local_heads = head_cols // HD
    normed_patches = layer_norm(vit_input.astype(jnp.float32), vit_ln_gain).astype(jnp.bfloat16)
    w_qkv_flat = w_qkv.reshape(patch_width, 3 * head_cols)
    projected = jnp.dot(
        gather(normed_patches, "tp", 0).reshape(tp_size * own_patches, patch_width),
        w_qkv_flat,
        preferred_element_type=jnp.float32,
    ).astype(jnp.bfloat16)
    group_patches = projected.shape[0]
    projected = projected.reshape(group_patches, 3, local_heads, HD)
    image_index = image_ids(image_lengths[0], group_patches)
    attended = attend(projected[:, 0], projected[:, 1], projected[:, 2], image_index).reshape(
        group_patches, head_cols
    )
    attn_part = jnp.dot(attended, w_proj, preferred_element_type=jnp.float32).astype(jnp.bfloat16)
    attn_sum = scatter_sum(
        attn_part.reshape(tp_size, own_patches, patch_width), "tp", jnp.float32, 1
    )
    vit_out = vit_input.astype(jnp.float32) + attn_sum
    own_tokens = own_patches // 4
    merged_in = (
        layer_norm(vit_out, merger_ln_gain)
        .astype(jnp.bfloat16)
        .reshape(own_tokens, 4 * patch_width)
    )
    expanded = jax.nn.gelu(
        jnp.dot(
            gather(merged_in, "tp", 2).reshape(tp_size * own_tokens, 4 * patch_width),
            merger_w1,
            preferred_element_type=jnp.float32,
        ),
        approximate=False,
    ).astype(jnp.bfloat16)
    slice_width = norm_gain.shape[0]
    hidden_width = gate_up_weight.shape[2]
    chunks = chunk_count(hidden_width)
    weight_rows = gate_up_weight.transpose(1, 2, 0).reshape(
        2, chunks, hidden_width // chunks, slice_width
    )
    down_rows = down_weight.reshape(chunks, hidden_width // chunks, slice_width)
    return decoder(
        expanded, positions[None, :], norm_gain[None, :], merger_w2, weight_rows, down_rows, 3
    )


def solution(mesh):
    return jax.shard_map(
        local,
        mesh=mesh,
        in_specs=(
            P(("seq", "tp"), None),
            P("seq", None),
            P(),
            P(),
            P(None, None, "tp"),
            P("tp", None),
            P(),
            P(None, "tp"),
            P("tp", None),
            P("seq"),
            P("seq", None, "tp"),
            P("tp", "seq"),
        ),
        out_specs=P("tp", "seq"),
        check_vma=False,
    )
```

time: 326 us -> 262 us (0.80)
  Pallas kernels: 274 us -> 239 us
  matrix products: 34 us -> 11.8 us
  other arithmetic: 15.2 us -> 7.85 us
    pallas_call x3 -> x1, Pallas kernels: 109 us -> 27.2 us  [scatter_sum(): pl.pallas_call(functools.partial(scatter_kernel, axis, n), out_shape=jax....]
    pallas_call x2 -> x1, Pallas kernels: 83.8 us -> 165 us  [decoder(): pl.pallas_call(functools.partial(decoder_kernel, parts), out_shape=jax.Sh...]
    pallas_call x3 -> x2, Pallas kernels: 80.9 us -> 47.5 us  [gather(): pl.pallas_call(functools.partial(gather_kernel, axis, n), out_shape=jax.S...]
    dot_general x3 -> x1, matrix products: 28 us -> 5.78 us  [local(): jnp.dot(gather(merged_in, 'tp', 2).reshape(tp_size * own_tokens, 4 * patc...]
where the time goes in v1:
time: 262 us; the launch traced here: 261 us
  Pallas kernels  239 us (91%)
  matrix products  11.8 us (5%)
  other arithmetic  7.85 us (3%)
    pallas_call x1, Pallas kernels, decoder(): pl.pallas_call(functools.partial(decoder_kernel, parts), out_shape=jax.Sh...  165 us
    pallas_call x2, Pallas kernels, gather(): pl.pallas_call(functools.partial(gather_kernel, axis, n), out_shape=jax.S...  47.5 us
    pallas_call x1, Pallas kernels, scatter_sum(): pl.pallas_call(functools.partial(scatter_kernel, axis, n), out_shape=jax....  27.2 us
    dot_general x1, matrix products, local(): jnp.dot(gather(merged_in, 'tp', 2).reshape(tp_size * own_tokens, 4 * patc...  5.78 us

profile of v1, /device:TPU:0, one launch (start us, length us, event | category | flops | bytes accessed | tf_op | source)
XLA Modules:
  0.0 261.5 jit_solution(16701012264575897045)
XLA Ops:
  0.0 1.1 convert_reduce_fusion
  1.2 1.1 fusion.7
  2.3 1.7 fusion.9.x_ref
  4.0 25.7 %gather0.1 = bf16[8,64,1280]{2,1,0:T(8,128)(2,1)} custom-call(bf16[64,1280]{1,0:T(8,128)(2,1)} %fusion.9.x_ref), custom_call_target="tpu_custom_call" | custom-call | tf_op jit(solution)/shard_map/gather0/pallas_call | solution.py:93
  29.7 0.0 copy-start.4
  29.7 2.1 convolution_convert_fusion.1
  31.9 0.2 reduce-window.8
  32.0 0.1 fusion.24
  32.1 0.2 broadcast_compare_fusion
  32.4 1.0 fusion.32
  33.4 1.3 convolution_convert_fusion.2
  34.6 0.0 copy-start
  34.6 0.0 copy-start.2
  34.6 1.6 convolution_convert_fusion
  36.3 27.2 %scatter_sum1.1 = f32[64,1280]{1,0:T(8,128)} custom-call(bf16[8,64,1280]{2,1,0:T(8,128)(2,1)} %bitcast.52), custom_call_target="tpu_custom_call" | custom-call | tf_op jit(solution)/shard_map/scatter_sum1/pallas_call | solution.py:158
  63.4 0.0 copy-done
  63.4 1.1 fusion.23
  64.6 1.2 multiply_reduce_fusion
  65.8 1.1 multiply_convert_fusion
  66.9 0.8 reshape.115.x_ref
  67.6 21.8 %gather2.1 = bf16[8,16,5120]{2,1,0:T(8,128)(2,1)} custom-call(bf16[16,5120]{1,0:T(8,128)(2,1)} %reshape.115.x_ref), custom_call_target="tpu_custom_call" | custom-call | tf_op jit(solution)/shard_map/gather2/pallas_call | solution.py:93
  89.5 5.8 %fusion.12.e_ref = bf16[128,640]{1,0:T(8,128)(2,1)} fusion(bf16[128,5120]{1,0:T(8,128)(2,1)} %bitcast.54, bf16[5120,640]{1,0:T(8,128)(2,1)} %param.19), kind=kOutput, calls=%fused_computation.23 | convolution fusion | flops 844185600 | bytes 8028160 | tf_op jit(solution)/shard_map/dot_general | solution.py:710
  95.3 164.5 %decoder.1 = bf16[64,2048]{1,0:T(8,128)(2,1)} custom-call(bf16[128,640]{1,0:T(8,128)(2,1)} %fusion.12.e_ref, s32[1,512]{1,0:T(1,128)} %bitcast.57, f32[1,2048]{1,0:T(1,128)} %bitcast.56, bf16[640,8192]{1,0:T(8,128)(2,1)} %w2_ref.1, bf16[2,7,528,2048]{3,2,1,0:T(8,128)(2,1)} %bitcast.50, bf16[7,528,2048]{2,1,0:T(8,128)(2,1)} %bitcast.51), custom_call_target="tpu_custom_call" | custom-call | tf_op jit(solution)/shard_map/decoder/pallas_call | solution.py:619
  259.8 1.7 copy.17
  (11 shorter events, 0.0 us)
Async XLA Ops:
  0.0 29.7 %copy-start.3 = (bf16[1280,3,160]{0,2,1:T(8,128)(2,1)S(1)}, bf16[1280,3,160]{0,2,1:T(8,128)(2,1)}, u32[]{:S(2)}) copy-start(bf16[1280,3,160]{0,2,1:T(8,128)(2,1)} %param.16) | copy-start | bytes 3686404
  29.7 2.2 copy-start.4
  33.3 1.3 copy-start.1
  34.6 28.8 %copy-start = (bf16[64,1280]{1,0:T(8,128)(2,1)S(1)}, bf16[64,1280]{1,0:T(8,128)(2,1)}, u32[]{:S(2)}) copy-start(bf16[64,1280]{1,0:T(8,128)(2,1)} %param.12) | copy-start | bytes 491524
  34.6 31.1 %copy-start.2 = (f32[1280]{0:T(1024)S(1)}, f32[1280]{0:T(1024)}, u32[]{:S(2)}) copy-start(f32[1280]{0:T(1024)} %param.18) | copy-start | bytes 15364

commit v2 on v1

v2 whole, which is shorter than its diff:
```python
import functools

import jax
import jax.numpy as jnp
from jax import lax
from jax.experimental import pallas as pl
from jax.experimental.pallas import tpu as pltpu
from jax.sharding import PartitionSpec as P

HD = 80
MESH = pl.DeviceIdType.MESH
LAG_C, LAG_D, LAG_E = 3, 5, 6
AT_PASS, AT_GATHER, AT_RELAY = (1, 2), (3, 3), (4, 5, 6)
VM = pl.BlockSpec(memory_space=pltpu.VMEM)


def factors(n):
    minor = max(d for d in range(1, n + 1) if n % d == 0 and d * d <= n)
    return n // minor, minor


def grid_peers(n_a, n_b, a, b):
    along_a = [lax.rem(a + da, n_a) * n_b + b for da in range(1, n_a)]
    along_b = [a * n_b + lax.rem(b + db, n_b) for db in range(1, n_b)]
    return along_a, along_b


def remote(src, dst, send_sem, recv_sem, axis, peer):
    return pltpu.make_async_remote_copy(
        src_ref=src,
        dst_ref=dst,
        send_sem=send_sem,
        recv_sem=recv_sem,
        device_id={axis: peer},
        device_id_type=MESH,
    )


class LineGather:
    def __init__(self, view, sems):
        n = lax.axis_size("tp")
        self.n_a, self.n_b = factors(n)
        me = lax.axis_index("tp")
        self.a, self.b = me // self.n_b, lax.rem(me, self.n_b)
        self.minors = grid_peers(self.n_a, self.n_b, self.a, self.b)[1]
        self.view, self.sems = view, sems

    def up(self, u, src):
        block = self.view(u, src * self.n_b + self.b)
        send, recv = self.sems["u_s"].at[u, src], self.sems["u_r"].at[u, src]
        return remote(block, block, send, recv, "tp", lax.rem(self.a + 1, self.n_a) * self.n_b + self.b)

    def down(self, u, src):
        block = self.view(u, src * self.n_b + self.b)
        send, recv = self.sems["d_s"].at[u, src], self.sems["d_r"].at[u, src]
        return remote(block, block, send, recv, "tp", lax.rem(self.a + self.n_a - 1, self.n_a) * self.n_b + self.b)

    def minor(self, u, src, db):
        block = self.view(u, src * self.n_b + self.b)
        send, recv = self.sems["m_s"].at[u, src, db - 1], self.sems["m_r"].at[u, src, db - 1]
        return remote(block, block, send, recv, "tp", self.minors[db - 1])

    def send(self, u, src, upward, downward):
        if upward:
            @pl.when(self.a < self.n_a - 1)
            def _():
                self.up(u, src).start()
        if downward:
            @pl.when(self.a > 0)
            def _():
                self.down(u, src).start()
        for db in range(1, self.n_b):
            self.minor(u, src, db).start()

    def start(self, u):
        self.send(u, self.a, True, True)

    def relay(self, u, k):
        @pl.when(self.a >= k)
        def _():
            self.up(u, self.a - k).wait_recv()
            self.send(u, self.a - k, True, False)

        @pl.when(self.a + k < self.n_a)
        def _():
            self.down(u, self.a + k).wait_recv()
            self.send(u, self.a + k, False, True)

    def finish(self, u):
        for src in range(self.n_a):
            for db in range(1, self.n_b):
                self.minor(u, src, db).wait()

            @pl.when(jnp.logical_and(src <= self.a, self.a < self.n_a - 1))
            def _():
                self.up(u, src).wait_send()

            @pl.when(jnp.logical_and(src >= self.a, self.a > 0))
            def _():
                self.down(u, src).wait_send()


def line_sems(units):
    m_a, m_b = factors(lax.axis_size("tp"))
    return {
        "u_s": (units, m_a), "u_r": (units, m_a), "d_s": (units, m_a), "d_r": (units, m_a),
        "m_s": (units, m_a, m_b), "m_r": (units, m_a, m_b),
    }


class ScatterSum:
    def __init__(self, part, r1, yb, r2, sems):
        m = lax.axis_size("tp")
        self.n_a, self.n_b = factors(m)
        me = lax.axis_index("tp")
        self.a, self.b = me // self.n_b, lax.rem(me, self.n_b)
        self.majors, self.minors = grid_peers(self.n_a, self.n_b, self.a, self.b)
        self.part, self.r1, self.yb, self.r2, self.sems = part, r1, yb, r2, sems
        self.order = sorted(range(1, self.n_a), key=lambda da: -min(da, self.n_a - da)) + [0]

    def minor(self, u, da, db):
        at = lax.rem(self.a + da, self.n_a) * self.n_b + lax.rem(self.b + db, self.n_b)
        send, recv = self.sems["rb_s"].at[u, da, db - 1], self.sems["rb_r"].at[u, da, db - 1]
        return remote(self.part.at[u, at], self.r1.at[u, da, db - 1], send, recv, "tp", self.minors[db - 1])

    def major(self, u, da):
        send, recv = self.sems["ra_s"].at[u, da - 1], self.sems["ra_r"].at[u, da - 1]
        return remote(self.yb.at[u, da - 1], self.r2.at[u, da - 1], send, recv, "tp", self.majors[da - 1])

    def start(self, u):
        for da in self.order:
            for db in range(1, self.n_b):
                self.minor(u, da, db).start()

    def arrived(self, u, da):
        total = self.part[u, lax.rem(self.a + da, self.n_a) * self.n_b + self.b].astype(jnp.float32)
        for db in range(1, self.n_b):
            self.minor(u, da, db).wait_recv()
            total = total + self.r1[u, da, db - 1].astype(jnp.float32)
        return total

    def forward(self, u):
        for da in self.order[:-1]:
            self.yb[u, da - 1] = self.arrived(u, da).astype(self.yb.dtype)
            self.major(u, da).start()

    def finish(self, u):
        total = self.arrived(u, 0)
        for da in self.order[:-1]:
            self.major(u, da).wait_recv()
            total = total + self.r2[u, da - 1].astype(jnp.float32)
        for da in self.order:
            for db in range(1, self.n_b):
                self.minor(u, da, db).wait_send()
        for da in self.order[:-1]:
            self.major(u, da).wait_send()
        return total


def scatter_sems(units):
    m_a, m_b = factors(lax.axis_size("tp"))
    return {"rb_s": (units, m_a, m_b), "rb_r": (units, m_a, m_b), "ra_s": (units, m_a), "ra_r": (units, m_a)}


def scatter_shapes(units, block, kind):
    m_a, m_b = factors(lax.axis_size("tp"))
    return {
        "part": ((units, m_a * m_b) + block, kind),
        "r1": ((units, m_a, m_b - 1) + block, kind),
        "yb": ((units, m_a - 1) + block, kind),
        "r2": ((units, m_a - 1) + block, kind),
    }


def normalize(values, gain):
    mean = jnp.mean(values, axis=-1, keepdims=True)
    centered = values - mean
    variance = jnp.mean(centered * centered, axis=-1, keepdims=True)
    return centered * lax.rsqrt(variance + 1e-06) * gain


V_BUFS = ("ag", "wq", "wp", "w1", "qkv", "att", "part", "r1", "yb", "r2", "vo", "vs", "ag2")
V_SEMS = ("wq", "wp", "w1", "u_s", "u_r", "d_s", "d_r", "m_s", "m_r", "rb_s", "rb_r", "ra_s", "ra_r")


def vision_kernel(vit_ref, len_ref, gain_ref, gain2_ref, wq_ref, wp_ref, w1_ref, out_ref, *scratch):
    buf = dict(zip(V_BUFS, scratch))
    sem = dict(zip(V_SEMS, scratch[len(V_BUFS):]))
    m = lax.axis_size("tp")
    m_a, m_b = factors(m)
    mt = lax.axis_index("tp")
    own, width = vit_ref.shape
    half = width // 2
    heads_wide = wp_ref.shape[0]
    f32, kind = jnp.float32, vit_ref.dtype
    loads = {
        k: pltpu.make_async_copy(ref, buf[k], sem[k]) for k, ref in (("wq", wq_ref), ("wp", wp_ref), ("w1", w1_ref))
    }
    for copy in loads.values():
        copy.start()
    majors, minors = grid_peers(m_a, m_b, mt // m_b, lax.rem(mt, m_b))
    barrier = pltpu.get_barrier_semaphore()
    for peer in majors + minors:
        pl.semaphore_signal(barrier, inc=1, device_id={"tp": peer}, device_id_type=MESH)

    ag, ag2, vo, part, qkv, att = (buf[k] for k in ("ag", "ag2", "vo", "part", "qkv", "att"))
    first = normalize(vit_ref[...].astype(f32), gain_ref[...]).astype(kind)
    for q in range(2):
        ag[q, mt] = first[:, q * half : (q + 1) * half]
    pl.semaphore_wait(barrier, len(majors) + len(minors))

    def unit_view(u, at):
        return ag.at[u, at]

    gather_one = LineGather(unit_view, sem)
    for u in range(2):
        gather_one.start(u)
    for k in range(1, m_a):
        for u in range(2):
            gather_one.relay(u, k)
    loads["wq"].wait()
    patches = m * own
    for u in range(2):
        gather_one.finish(u)
        piece = lax.dot_general(
            buf["wq"][:, u * half : (u + 1) * half],
            ag[u].reshape(patches, half),
            (((1,), (1,)), ((), ())),
            preferred_element_type=f32,
        )
        if u == 0:
            qkv[...] = piece
        else:
            qkv[...] += piece

    ends = jnp.zeros((1, 1), jnp.int32)
    ids_row = jnp.zeros((1, patches), jnp.int32)
    ids_col = jnp.zeros((patches, 1), jnp.int32)
    at_row = lax.broadcasted_iota(jnp.int32, (1, patches), 1)
    at_col = lax.broadcasted_iota(jnp.int32, (patches, 1), 0)
    for image in range(len_ref.shape[1]):
        ends = ends + len_ref[:, image : image + 1]
        ids_row = ids_row + (at_row >= ends * 4).astype(jnp.int32)
        ids_col = ids_col + (at_col >= ends * 4).astype(jnp.int32)
    same = ids_col == ids_row
    for head in range(heads_wide // HD):
        query, keys, values = (
            qkv[c * heads_wide + head * HD : c * heads_wide + (head + 1) * HD].astype(kind) for c in range(3)
        )
        scores = lax.dot_general(keys, query, (((0,), (0,)), ((), ())), preferred_element_type=f32) * HD ** (-0.5)
        scores = jnp.where(same, scores, -1e30)
        top = jnp.max(scores, axis=0, keepdims=True)
        expo = jnp.exp(scores - top)
        weights = (expo / jnp.sum(expo, axis=0, keepdims=True)).astype(kind)
        att[head * HD : (head + 1) * HD] = jnp.dot(values, weights, preferred_element_type=f32).astype(kind)
    loads["wp"].wait()
    total = ScatterSum(part, buf["r1"], buf["yb"], buf["r2"], sem)
    for u in range(2):
        piece = lax.dot_general(
            att[...], buf["wp"][:, u * half : (u + 1) * half], (((0,), (0,)), ((), ())), preferred_element_type=f32
        )
        part[u] = piece.astype(kind).reshape(m, own, half)
        total.start(u)
    for u in range(2):
        total.forward(u)
    for u in range(2):
        at = slice(u * half, (u + 1) * half)
        vo[:, at] = vit_ref[:, at].astype(f32) + total.finish(u)
    second = normalize(vo[...], gain2_ref[...])
    for k in range(width // 128):
        buf["vs"][k] = second[:, k * 128 : (k + 1) * 128]
    tokens = own // 4

    def merged_view(u, at):
        return ag2.at[u - 2, :, at]

    gather_two = LineGather(merged_view, sem)
    for q in range(2):
        for j in range(4):
            for k in range(half // 128):
                ag2[q, j, mt, :, k * 128 : (k + 1) * 128] = buf["vs"][
                    q * half // 128 + k, pl.ds(j, tokens, stride=4), :
                ].astype(kind)
        gather_two.start(q + 2)
    for k in range(1, m_a):
        for u in range(2):
            gather_two.relay(u + 2, k)
    loads["w1"].wait()
    expanded = None
    for u in range(2):
        gather_two.finish(u + 2)
        for j in range(4):
            at = j * width + u * half
            piece = jnp.dot(
                ag2[u, j].reshape(m * tokens, half), buf["w1"][at : at + half], preferred_element_type=f32
            )
            expanded = piece if expanded is None else expanded + piece
    out_ref[...] = (0.5 * expanded * (1.0 + lax.erf(expanded * 0.5**0.5))).astype(kind)


def vision(vit, lengths, gain, gain2, w_qkv, w_proj, w1, collective_id):
    m = lax.axis_size("tp")
    own, width = vit.shape
    half, kind, f32 = width // 2, vit.dtype, jnp.float32
    heads_wide = w_proj.shape[0]
    shapes = {
        "ag": ((2, m, own, half), kind),
        "wq": (w_qkv.shape, kind),
        "wp": (w_proj.shape, kind),
        "w1": (w1.shape, kind),
        "qkv": ((3 * heads_wide, m * own), f32),
        "att": ((heads_wide, m * own), kind),
        "vo": ((own, width), f32),
        "vs": ((width // 128, own, 128), f32),
        "ag2": ((2, 4, m, own // 4, half), kind),
    }
    shapes |= scatter_shapes(2, (own, half), kind)
    sems = {"wq": (), "wp": (), "w1": ()} | line_sems(4) | scatter_sems(2)
    anywhere = pl.BlockSpec(memory_space=pl.ANY)
    return pl.pallas_call(
        vision_kernel,
        out_shape=jax.ShapeDtypeStruct((m * own // 4, w1.shape[1]), kind),
        in_specs=[VM, VM, VM, VM, anywhere, anywhere, anywhere],
        out_specs=VM,
        scratch_shapes=[pltpu.VMEM(*shapes[k]) for k in V_BUFS]
        + [pltpu.SemaphoreType.DMA(sems[k]) if sems[k] else pltpu.SemaphoreType.DMA for k in V_SEMS],
        name="vision",
        compiler_params=pltpu.CompilerParams(
            collective_id=collective_id, has_side_effects=True, vmem_limit_bytes=60_000_000
        ),
    )(vit, lengths, gain, gain2, w_qkv, w_proj, w1)


SEMS = (
    "w2", "w", "d", "ea_s", "ea_r", "eb_s", "eb_r", "q_s", "q_r", "p_s", "p_r", "y_s", "y_r", "h_s", "h_r",
    "o_s", "b_r", "rb_s", "rb_r", "ra_s", "ra_r", "u_s", "u_r", "d_s", "d_r", "m_s", "m_r",
)
BUFS = (
    "ex", "w2s", "part", "r1", "yb", "r2", "tok", "nrm", "sqa", "rq", "inv", "held", "dheld", "gu", "pin",
    "keep", "yx", "rx", "hid", "acc",
)


def decoder_kernel(parts, e_ref, pos_ref, gain_ref, w2_ref, w_ref, d_ref, out_ref, *scratch):
    buf = dict(zip(BUFS, scratch))
    sem = dict(zip(SEMS, scratch[len(BUFS):]))
    n, m = lax.axis_size("seq"), lax.axis_size("tp")
    (n_a, n_b), (m_a, m_b) = factors(n), factors(m)
    me, mt = lax.axis_index("seq"), lax.axis_index("tp")
    a, b = me // n_b, lax.rem(me, n_b)
    ta, tb = mt // m_b, lax.rem(mt, m_b)
    x_peers, core_peers = grid_peers(n_a, n_b, a, b)
    t_major, t_minor = grid_peers(m_a, m_b, ta, tb)
    partner = core_peers[0]
    chunks, rows, depth = w_ref.shape[1:]
    steps = parts * chunks
    owned = steps // n_b
    count = n_a * 128
    block = count // m
    half = depth // 2

    def to(axis, src, dst, s, r, peer):
        return remote(src, dst, s, r, axis, peer)

    def lanes(owner):
        return pl.ds(pl.multiple_of(owner * 128, 128), 128)

    w2_load = pltpu.make_async_copy(
        w2_ref.at[:, pl.ds(pl.multiple_of(me * depth, depth), depth)], buf["w2s"], sem["w2"]
    )

    def w_load(i):
        slot = lax.rem(i, 2)
        return pltpu.make_async_copy(w_ref.at[:, lax.rem(i, chunks)], buf["held"].at[slot], sem["w"].at[slot])

    def d_load(i):
        slot = lax.rem(i, 2)
        return pltpu.make_async_copy(d_ref.at[lax.rem(i, chunks)], buf["dheld"].at[slot], sem["d"].at[slot])

    w2_load.start()
    w_load(0).start()

    barrier = pltpu.get_barrier_semaphore()
    everyone = [("seq", lax.rem(me + d, n)) for d in range(1, n)]
    everyone += [("tp", peer) for peer in t_major + t_minor]
    for axis, peer in everyone:
        pl.semaphore_signal(barrier, inc=1, device_id={axis: peer}, device_id_type=MESH)
    pl.semaphore_wait(barrier, len(everyone))

    ex = buf["ex"]
    e_a = [
        to("seq", e_ref, ex.at[me], sem["ea_s"].at[da - 1], sem["ea_r"].at[da - 1], x_peers[da - 1])
        for da in range(1, n_a)
    ]
    e_b = [to("seq", e_ref, ex.at[me], sem["eb_s"].at[0], sem["eb_r"].at[0], partner)]
    for copy in e_a + e_b:
        copy.start()
    ex[me] = e_ref[...]
    for da in range(1, n_a):
        e_a[da - 1].wait_recv()
        source = ex.at[lax.rem(a - da + n_a, n_a) * n_b + b]
        copy = to("seq", source, source, sem["eb_s"].at[da], sem["eb_r"].at[da], partner)
        copy.start()
        e_b.append(copy)
    for copy in e_b:
        copy.wait()
    for copy in e_a:
        copy.wait_send()

    part, tok = buf["part"], buf["tok"]
    sums = ScatterSum(part, buf["r1"], buf["yb"], buf["r2"], sem)
    tokens_of = LineGather(lambda u, at: tok.at[u, at], sem)

    def ag_start(u):
        tok[u, mt] = sums.finish(u).astype(tok.dtype)
        tokens_of.start(u)

    rq, inv, sqa, nrm = buf["rq"], buf["inv"], buf["sqa"], buf["nrm"]

    def squares(h, d):
        return to(
            "seq", rq.at[h, me], rq.at[h, me], sem["q_s"].at[h, d - 1], sem["q_r"].at[h, d - 1], lax.rem(me + d, n)
        )

    def ag_finish(h):
        tokens_of.finish(h)
        first = lax.rem(h, 2) * half

        def rows_of(t, carry):
            values = tok[h, t].astype(jnp.float32)
            at = pl.ds(pl.multiple_of(t * block, block), block)
            cols = pl.ds(pl.multiple_of(first, 128), half)
            nrm[at, cols] = (values * gain_ref[:, cols]).astype(nrm.dtype)
            total = values[:, :128] * values[:, :128]
            for k in range(1, half // 128):
                piece = values[:, k * 128 : (k + 1) * 128]
                total = total + piece * piece
            sqa[lax.rem(h, 2), at] = total
            return carry

        lax.fori_loop(0, m, rows_of, 0)

    def ag_both(h):
        ag_finish(2 * h)
        ag_finish(2 * h + 1)
        squared = jnp.sum(jnp.transpose(sqa[0] + sqa[1]), axis=0, keepdims=True)
        rq[h, me] = jnp.broadcast_to(squared, (8, count))
        for d in range(1, n):
            squares(h, d).start()

    def inverse(h):
        for d in range(1, n):
            squares(h, d).wait()
        total = rq[h, 0]
        for s in range(1, n):
            total = total + rq[h, s]
        inv[h] = lax.rsqrt(total / (depth * n) + 1e-06)

    w2_load.wait()
    for h in range(parts):
        row = lax.broadcasted_iota(jnp.int32, (count, pos_ref.shape[1]), 0)
        slot = lax.shift_right_logical(row, block.bit_length() - 1) * (block * (parts - 1)) + row + h * block
        pick = (slot == pos_ref[...]).astype(jnp.bfloat16)
        moved = jnp.dot(
            pick, ex[...].reshape(pos_ref.shape[1], ex.shape[2]), preferred_element_type=jnp.float32
        ).astype(jnp.bfloat16)
        width = min(512, half)
        for k in range(depth // width):
            piece = jnp.dot(
                moved, buf["w2s"][:, k * width : (k + 1) * width], preferred_element_type=jnp.float32
            ).astype(part.dtype)
            q, at = k * width // half, k * width % half
            part[2 * h + q, :, :, at : at + width] = piece.reshape(m, block, width)
            if h == 0 and at + width == half:
                sums.start(q)
    sums.forward(0)
    sums.forward(1)
    ag_start(0)
    ag_start(1)
    for k in range(1, m_a):
        for u in range(2):
            tokens_of.relay(u, k)
    if parts > 1:
        sums.start(2)
        sums.start(3)
    ag_both(0)

    gu, pin, keep, yx, rx, hid, acc = (buf[k] for k in ("gu", "pin", "keep", "yx", "rx", "hid", "acc"))

    def owner(i):
        return lax.rem(i, n_b) == b

    def to_owner(i):
        return to("seq", gu.at[lax.rem(i, 2)], pin.at[i // n_b], sem["p_s"].at[i // n_b], sem["p_r"].at[i // n_b], partner)

    def to_x(i, da):
        o = i // n_b
        return to(
            "seq", yx.at[o, da - 1], rx.at[o, da - 1], sem["y_s"].at[o, da - 1], sem["y_r"].at[o, da - 1], x_peers[da - 1]
        )

    def hid_x(i, da):
        target = hid.at[i, :, lanes(a)]
        return to("seq", target, target, sem["h_s"].at[i, da - 1], sem["h_r"].at[i, da - 1], x_peers[da - 1])

    def hid_core(i, da):
        target = hid.at[i, :, lanes(lax.rem(a - da + n_a, n_a))]
        return to("seq", target, target, sem["o_s"].at[i, da], sem["b_r"].at[i, da], partner)

    def stage_a(i):
        w_load(i).wait()

        @pl.when(i + 1 < steps)
        def _():
            w_load(i + 1).start()

        for half in range(2):
            gu[lax.rem(i, 2), half] = lax.dot_general(
                buf["held"][lax.rem(i, 2), half],
                nrm[...],
                (((1,), (1,)), ((), ())),
                preferred_element_type=jnp.float32,
            ).astype(gu.dtype)

        @pl.when(jnp.logical_not(owner(i)))
        def _():
            to_owner(i).start()

    def stage_b(i):
        o = i // n_b

        @pl.when(owner(i))
        def _():
            to_owner(i).wait_recv()

            def both(da):
                at = lanes(lax.rem(a + da, n_a))
                return gu[lax.rem(i, 2), :, :, at].astype(jnp.float32) + pin[o, :, :, at].astype(jnp.float32)

            for da in range(1, n_a):
                yx[o, da - 1] = both(da).astype(yx.dtype)
                to_x(i, da).start()
            keep[lax.rem(o, 2)] = both(0)

        @pl.when(jnp.logical_not(owner(i)))
        def _():
            to_owner(i).wait_send()

    def stage_c(i):
        o, h = i // n_b, i // chunks

        @pl.when(lax.rem(i, chunks) == 0)
        def _():
            inverse(h)

        @pl.when(owner(i))
        def _():
            total = keep[lax.rem(o, 2)]
            for da in range(1, n_a):
                to_x(i, da).wait()
                total = total + rx[o, da - 1].astype(jnp.float32)
            total = total * inv[h, 0:1, lanes(a)]
            hid[i, :, lanes(a)] = (jax.nn.silu(total[0]) * total[1]).astype(hid.dtype)
            for da in range(1, n_a):
                hid_x(i, da).start()
            hid_core(i, 0).start()

    def stage_d(i):
        @pl.when(owner(i))
        def _():
            for da in range(1, n_a):
                hid_x(i, da).wait()
                hid_core(i, da).start()

    def stage_e(i):
        c, h = lax.rem(i, chunks), i // chunks

        @pl.when(owner(i))
        def _():
            for da in range(n_a):
                hid_core(i, da).wait_send()

        @pl.when(jnp.logical_not(owner(i)))
        def _():
            for da in range(n_a):
                hid_core(i, da).wait_recv()

        d_load(i).wait()
        width = min(512, depth)
        left = hid[i]
        for k in range(depth // width):
            at = slice(k * width, (k + 1) * width)
            piece = lax.dot_general(
                left, buf["dheld"][lax.rem(i, 2), :, at], (((0,), (0,)), ((), ())), preferred_element_type=jnp.float32
            )

            @pl.when(c == 0)
            def _():
                acc[:, at] = piece

            @pl.when(c > 0)
            def _():
                acc[:, at] += piece

        @pl.when(c == chunks - 1)
        def _():
            for q in range(2):
                u = 2 * parts + 2 * h + q
                part[u] = acc[:, q * half : (q + 1) * half].astype(part.dtype).reshape(m, block, half)
                sums.start(u)

    def down_pass(h):
        sums.forward(2 * parts + 2 * h)
        sums.forward(2 * parts + 2 * h + 1)

    def output(h):
        at = pl.ds(pl.multiple_of(h * block, block), block)
        for q in range(2):
            total = sums.finish(2 * parts + 2 * h + q)
            out_ref[at, q * half : (q + 1) * half] = (
                tok[2 * h + q, mt].astype(jnp.float32) + total
            ).astype(out_ref.dtype)

    def iteration(i, carry):
        def when(lag, fn):
            @pl.when(jnp.logical_and(i >= lag, i - lag < steps))
            def _():
                fn(i - lag)

        h, k = i // chunks, lax.rem(i, chunks)
        more = h + 1 < parts

        def at_step(step, q, fn):
            @pl.when(jnp.logical_and(more, k == step * chunks // 7))
            def _():
                fn(2 * h + 2 + q)

        @pl.when(jnp.logical_and(jnp.logical_and(i > 0, i < steps), k == 0))
        def _():
            @pl.when(more)
            def _():
                sums.start(2 * h + 2)
                sums.start(2 * h + 3)

            ag_both(h)

        when(LAG_E - 1, lambda j: d_load(j).start())
        when(0, stage_a)
        when(1, stage_b)
        when(LAG_C, stage_c)
        when(LAG_D, stage_d)
        for q in range(2):
            at_step(AT_PASS[q], q, sums.forward)
        for q in range(2):
            at_step(AT_GATHER[q], q, ag_start)
        for hop in range(1, m_a):
            for q in range(2):
                at_step(AT_RELAY[min(hop - 1, 2)], q, lambda u, hop=hop: tokens_of.relay(u, hop))
        when(LAG_E, stage_e)

        def later(lag, fn):
            @pl.when(jnp.logical_and(i - lag >= chunks, jnp.logical_and(lax.rem(i - lag + chunks, chunks) == 0, i - lag < steps)))
            def _():
                fn((i - lag) // chunks - 1)

        later(LAG_E + 1, down_pass)
        later(LAG_E + 3, output)
        return carry

    lax.fori_loop(0, steps + LAG_E, iteration, 0)
    down_pass(parts - 1)
    output(parts - 1)


def decoder(expanded, positions, gain, w2, weight, down, collective_id):
    n, m = lax.axis_size("seq"), lax.axis_size("tp")
    (n_a, n_b), (m_a, m_b) = factors(n), factors(m)
    _, chunks, rows, depth = weight.shape
    tokens = positions.shape[1]
    count = n_a * 128
    parts = tokens // count
    steps = parts * chunks
    block = count // m
    assert n_b == 2 and steps % 2 == 0 and chunks >= 7
    kind, f32 = expanded.dtype, jnp.float32
    shapes = {
        "ex": ((n,) + expanded.shape, kind),
        "w2s": ((w2.shape[0], depth), kind),
        "tok": ((2 * parts, m, block, depth // 2), kind),
        "nrm": ((count, depth), kind),
        "sqa": ((2, count, 128), f32),
        "rq": ((parts, n, 8, count), f32),
        "inv": ((parts, 8, count), f32),
        "held": ((2, 2, rows, depth), kind),
        "dheld": ((2, rows, depth), kind),
        "gu": ((2, 2, rows, count), kind),
        "pin": ((steps // 2, 2, rows, count), kind),
        "keep": ((2, 2, rows, 128), f32),
        "yx": ((steps // 2, n_a - 1, 2, rows, 128), kind),
        "rx": ((steps // 2, n_a - 1, 2, rows, 128), kind),
        "hid": ((steps, rows, count), kind),
        "acc": ((count, depth), f32),
    }
    shapes |= scatter_shapes(4 * parts, (block, depth // 2), kind)
    sems = {
        "w2": (),
        "w": (2,),
        "d": (2,),
        "ea_s": (n_a,),
        "ea_r": (n_a,),
        "eb_s": (n_a,),
        "eb_r": (n_a,),
        "q_s": (parts, n),
        "q_r": (parts, n),
        "p_s": (steps // 2,),
        "p_r": (steps // 2,),
        "y_s": (steps // 2, n_a),
        "y_r": (steps // 2, n_a),
        "h_s": (steps, n_a),
        "h_r": (steps, n_a),
        "o_s": (steps, n_a),
        "b_r": (steps, n_a),
    }
    sems |= scatter_sems(4 * parts) | line_sems(2 * parts)
    anywhere = pl.BlockSpec(memory_space=pl.ANY)
    return pl.pallas_call(
        functools.partial(decoder_kernel, parts),
        out_shape=jax.ShapeDtypeStruct((tokens // m, depth), kind),
        in_specs=[VM, VM, VM, anywhere, anywhere, anywhere],
        out_specs=VM,
        scratch_shapes=[pltpu.VMEM(*shapes[k]) for k in BUFS]
        + [pltpu.SemaphoreType.DMA(sems[k]) if sems[k] else pltpu.SemaphoreType.DMA for k in SEMS],
        name="decoder",
        compiler_params=pltpu.CompilerParams(
            collective_id=collective_id, has_side_effects=True, vmem_limit_bytes=67_000_000
        ),
    )(expanded, positions, gain, w2, weight, down)


def chunk_count(rows):
    for count in (7, 6, 4, 3, 2):
        if rows % (count * 8) == 0:
            return count
    return 1


def local(
    vit_input,
    image_lengths,
    positions,
    vit_ln_gain,
    w_qkv,
    w_proj,
    merger_ln_gain,
    merger_w1,
    merger_w2,
    norm_gain,
    gate_up_weight,
    down_weight,
):
    width, _, head_cols = w_qkv.shape
    expanded = vision(
        vit_input,
        image_lengths,
        vit_ln_gain[None, :],
        merger_ln_gain[None, :],
        w_qkv.transpose(1, 2, 0).reshape(3 * head_cols, width),
        w_proj,
        merger_w1,
        0,
    )
    slice_width = norm_gain.shape[0]
    hidden_width = gate_up_weight.shape[2]
    chunks = chunk_count(hidden_width)
    weight_rows = gate_up_weight.transpose(1, 2, 0).reshape(
        2, chunks, hidden_width // chunks, slice_width
    )
    down_rows = down_weight.reshape(chunks, hidden_width // chunks, slice_width)
    return decoder(
        expanded, positions[None, :], norm_gain[None, :], merger_w2, weight_rows, down_rows, 3
    )


def solution(mesh):
    return jax.shard_map(
        local,
        mesh=mesh,
        in_specs=(
            P(("seq", "tp"), None),
            P("seq", None),
            P(),
            P(),
            P(None, None, "tp"),
            P("tp", None),
            P(),
            P(None, "tp"),
            P("tp", None),
            P("seq"),
            P("seq", None, "tp"),
            P("tp", "seq"),
        ),
        out_specs=P("tp", "seq"),
        check_vma=False,
    )
```

time: 262 us -> 206 us (0.79)
  Pallas kernels: 239 us -> 202 us
  matrix products: 11.8 us -> 0 us
  other arithmetic: 7.85 us -> 0 us
    pallas_call x1, Pallas kernels: 165 us -> 140 us  [decoder(): pl.pallas_call(functools.partial(decoder_kernel, parts), out_shape=jax.Sh...]
    pallas_call x3 -> x1, Pallas kernels: 74.7 us -> 61.3 us  [vision(): pl.pallas_call(vision_kernel, out_shape=jax.ShapeDtypeStruct((m * own //...]
    dot_general x4 -> x0, matrix products: 10.8 us -> none  [the longest x1 5.78 us: local(): jnp.dot(gather(merged_in, 'tp', 2).reshape(tp_size * own_tokens, 4 * patc...]
    reduce_sum x5 -> x0, other arithmetic: 4.64 us -> none  [the longest x2 2.31 us: layer_norm(): variance = jnp.mean(centered * centered, axis=-1, keepdims=True)]
    convert_element_type x2 -> x0, other arithmetic: 2.79 us -> none  [the longest x1 1.71 us: local(): layer_norm(vit_input.astype(jnp.float32), vit_ln_gain).astype(jnp.bfloat16)]
where the time goes in v2:
time: 206 us
  Pallas kernels  202 us (98%)
  local copies, waits for them, and re-layouts  4.26 us (2%)
    pallas_call x1, Pallas kernels, decoder(): pl.pallas_call(functools.partial(decoder_kernel, parts), out_shape=jax.Sh...  140 us
    pallas_call x1, Pallas kernels, vision(): pl.pallas_call(vision_kernel, out_shape=jax.ShapeDtypeStruct((m * own //...  61.3 us

profile of v2, /device:TPU:0, one launch (start us, length us, event | category | flops | bytes accessed | tf_op | source)
XLA Modules:
  0.0 205.8 jit_solution(4763745923950152841)
XLA Ops:
  0.0 1.3 broadcast_in_dim.12.gain_ref
  1.3 1.3 broadcast_in_dim.13.gain2_ref
  2.6 61.3 %vision.1.e_ref = bf16[128,640]{1,0:T(8,128)(2,1)} custom-call(bf16[64,1280]{1,0:T(8,128)(2,1)} %vit_ref.1, s32[1,2]{1,0:T(1,128)} %len_ref.1, f32[1,1280]{1,0:T(1,128)} %broadcast_in_dim.12.gain_ref, f32[1,1280]{1,0:T(1,128)} %broadcast_in_dim.13.gain2_ref, bf16[480,1280]{1,0:T(8,128)(2,1)} %bitcast.11, bf16[160,1280]{1,0:T(8,128)(2,1)} %wp_ref.1, ...), custom_call_target="tpu_custom_call" | custom-call | tf_op jit(solution)/shard_map/vision/pallas_call | solution.py:320
  63.9 140.2 %decoder.1 = bf16[64,2048]{1,0:T(8,128)(2,1)} custom-call(bf16[128,640]{1,0:T(8,128)(2,1)} %vision.1.e_ref, s32[1,512]{1,0:T(1,128)} %bitcast.13, f32[1,2048]{1,0:T(1,128)} %bitcast.12, bf16[640,8192]{1,0:T(8,128)(2,1)} %w2_ref.1, bf16[2,7,528,2048]{3,2,1,0:T(8,128)(2,1)} %bitcast.9, bf16[7,528,2048]{2,1,0:T(8,128)(2,1)} %bitcast.10), custom_call_target="tpu_custom_call" | custom-call | tf_op jit(solution)/shard_map/decoder/pallas_call | solution.py:726
  204.1 1.7 copy.14

commit v3 on v2

v3 whole, which is shorter than its diff:
```python
import functools

import jax
import jax.numpy as jnp
from jax import lax
from jax.experimental import pallas as pl
from jax.experimental.pallas import tpu as pltpu
from jax.sharding import PartitionSpec as P

HD = 80
MESH = pl.DeviceIdType.MESH
LAG_C, LAG_D, LAG_E = 3, 5, 6
AT_PASS, AT_GATHER, AT_RELAY = (0, 1), (2, 3), (2, 3)
VM = pl.BlockSpec(memory_space=pltpu.VMEM)


def factors(n):
    minor = max(d for d in range(1, n + 1) if n % d == 0 and d * d <= n)
    return n // minor, minor


def grid_peers(n_a, n_b, a, b):
    along_a = [lax.rem(a + da, n_a) * n_b + b for da in range(1, n_a)]
    along_b = [a * n_b + lax.rem(b + db, n_b) for db in range(1, n_b)]
    return along_a, along_b


def remote(src, dst, send_sem, recv_sem, axis, peer):
    return pltpu.make_async_remote_copy(
        src_ref=src,
        dst_ref=dst,
        send_sem=send_sem,
        recv_sem=recv_sem,
        device_id={axis: peer},
        device_id_type=MESH,
    )


class LineGather:
    def __init__(self, view, sems):
        n = lax.axis_size("tp")
        self.n_a, self.n_b = factors(n)
        me = lax.axis_index("tp")
        self.a, self.b = me // self.n_b, lax.rem(me, self.n_b)
        self.minors = grid_peers(self.n_a, self.n_b, self.a, self.b)[1]
        self.view, self.sems = view, sems

    def up(self, u, src):
        block = self.view(u, src * self.n_b + self.b)
        send, recv = self.sems["u_s"].at[u, src], self.sems["u_r"].at[u, src]
        return remote(block, block, send, recv, "tp", lax.rem(self.a + 1, self.n_a) * self.n_b + self.b)

    def down(self, u, src):
        block = self.view(u, src * self.n_b + self.b)
        send, recv = self.sems["d_s"].at[u, src], self.sems["d_r"].at[u, src]
        return remote(block, block, send, recv, "tp", lax.rem(self.a + self.n_a - 1, self.n_a) * self.n_b + self.b)

    def minor(self, u, src, db):
        block = self.view(u, src * self.n_b + self.b)
        send, recv = self.sems["m_s"].at[u, src, db - 1], self.sems["m_r"].at[u, src, db - 1]
        return remote(block, block, send, recv, "tp", self.minors[db - 1])

    def send(self, u, src, upward, downward):
        if upward:
            @pl.when(self.a < self.n_a - 1)
            def _():
                self.up(u, src).start()
        if downward:
            @pl.when(self.a > 0)
            def _():
                self.down(u, src).start()
        for db in range(1, self.n_b):
            self.minor(u, src, db).start()

    def start(self, u):
        self.send(u, self.a, True, True)

    def relay(self, u, k):
        @pl.when(self.a >= k)
        def _():
            self.up(u, self.a - k).wait_recv()
            self.send(u, self.a - k, True, False)

        @pl.when(self.a + k < self.n_a)
        def _():
            self.down(u, self.a + k).wait_recv()
            self.send(u, self.a + k, False, True)

    def finish(self, u):
        for src in range(self.n_a):
            for db in range(1, self.n_b):
                self.minor(u, src, db).wait()

            @pl.when(jnp.logical_and(src <= self.a, self.a < self.n_a - 1))
            def _():
                self.up(u, src).wait_send()

            @pl.when(jnp.logical_and(src >= self.a, self.a > 0))
            def _():
                self.down(u, src).wait_send()


def line_sems(units):
    m_a, m_b = factors(lax.axis_size("tp"))
    return {
        "u_s": (units, m_a), "u_r": (units, m_a), "d_s": (units, m_a), "d_r": (units, m_a),
        "m_s": (units, m_a, m_b), "m_r": (units, m_a, m_b),
    }


class ScatterSum:
    def __init__(self, part, r1, yb, r2, sems):
        m = lax.axis_size("tp")
        self.n_a, self.n_b = factors(m)
        me = lax.axis_index("tp")
        self.a, self.b = me // self.n_b, lax.rem(me, self.n_b)
        self.majors, self.minors = grid_peers(self.n_a, self.n_b, self.a, self.b)
        self.part, self.r1, self.yb, self.r2, self.sems = part, r1, yb, r2, sems
        self.order = sorted(range(1, self.n_a), key=lambda da: -min(da, self.n_a - da)) + [0]

    def slot(self, u):
        return lax.rem(u, self.part.shape[0])

    def minor(self, u, da, db):
        at = lax.rem(self.a + da, self.n_a) * self.n_b + lax.rem(self.b + db, self.n_b)
        send, recv = self.sems["rb_s"].at[u, da, db - 1], self.sems["rb_r"].at[u, da, db - 1]
        return remote(self.part.at[self.slot(u), at], self.r1.at[u, da, db - 1], send, recv, "tp", self.minors[db - 1])

    def major(self, u, da):
        send, recv = self.sems["ra_s"].at[u, da - 1], self.sems["ra_r"].at[u, da - 1]
        return remote(self.yb.at[self.slot(u), da - 1], self.r2.at[u, da - 1], send, recv, "tp", self.majors[da - 1])

    def start(self, u):
        for da in self.order:
            for db in range(1, self.n_b):
                self.minor(u, da, db).start()

    def arrived(self, u, da):
        total = self.part[self.slot(u), lax.rem(self.a + da, self.n_a) * self.n_b + self.b].astype(jnp.float32)
        for db in range(1, self.n_b):
            self.minor(u, da, db).wait_recv()
            total = total + self.r1[u, da, db - 1].astype(jnp.float32)
        return total

    def forward(self, u):
        for da in self.order[:-1]:
            self.yb[self.slot(u), da - 1] = self.arrived(u, da).astype(self.yb.dtype)
            self.major(u, da).start()

    def finish(self, u):
        total = self.arrived(u, 0)
        for da in self.order[:-1]:
            self.major(u, da).wait_recv()
            total = total + self.r2[u, da - 1].astype(jnp.float32)
        for da in self.order:
            for db in range(1, self.n_b):
                self.minor(u, da, db).wait_send()
        for da in self.order[:-1]:
            self.major(u, da).wait_send()
        return total


def scatter_sems(units):
    m_a, m_b = factors(lax.axis_size("tp"))
    return {"rb_s": (units, m_a, m_b), "rb_r": (units, m_a, m_b), "ra_s": (units, m_a), "ra_r": (units, m_a)}


def scatter_shapes(units, slots, block, kind):
    m_a, m_b = factors(lax.axis_size("tp"))
    return {
        "part": ((slots, m_a * m_b) + block, kind),
        "r1": ((units, m_a, m_b - 1) + block, kind),
        "yb": ((slots, m_a - 1) + block, kind),
        "r2": ((units, m_a - 1) + block, kind),
    }


def lane_rows(vector):
    return vector.reshape(-1, 128)


def one_row(ref, first=0, count=None):
    count = ref.shape[0] if count is None else count
    return jnp.concatenate([ref[pl.ds(first + k, 1)] for k in range(count)], axis=1)


def normalize(values, gain):
    mean = jnp.mean(values, axis=-1, keepdims=True)
    centered = values - mean
    variance = jnp.mean(centered * centered, axis=-1, keepdims=True)
    return centered * lax.rsqrt(variance + 1e-06) * gain


def keyed(prefix, named):
    return {prefix + k: v for k, v in named.items()}


def under(prefix, named):
    return {k[len(prefix):]: v for k, v in named.items() if k.startswith(prefix)}


def vision_stage(vit_ref, len_ref, gain_ref, gain2_ref, loads, buf, sem, enter, emit):
    m = lax.axis_size("tp")
    m_a, m_b = factors(m)
    mt = lax.axis_index("tp")
    own, width = vit_ref.shape
    half = width // 2
    heads_wide = buf["wp"].shape[0]
    f32, kind = jnp.float32, vit_ref.dtype
    ag, ag2, vo, part, qkv, att = (buf[k] for k in ("ag", "ag2", "vo", "part", "qkv", "att"))
    first = normalize(vit_ref[...].astype(f32), one_row(gain_ref)).astype(kind)
    for q in range(2):
        ag[q, mt] = first[:, q * half : (q + 1) * half]
    enter()

    def unit_view(u, at):
        return ag.at[u, at]

    gather_one = LineGather(unit_view, sem)
    for u in range(2):
        gather_one.start(u)
    for k in range(1, m_a):
        for u in range(2):
            gather_one.relay(u, k)
    loads["wq"].wait()
    patches = m * own
    for u in range(2):
        gather_one.finish(u)
        piece = lax.dot_general(
            buf["wq"][:, u * half : (u + 1) * half],
            ag[u].reshape(patches, half),
            (((1,), (1,)), ((), ())),
            preferred_element_type=f32,
        )
        if u == 0:
            qkv[...] = piece
        else:
            qkv[...] += piece

    ends = jnp.zeros((1, 1), jnp.int32)
    ids_row = jnp.zeros((1, patches), jnp.int32)
    ids_col = jnp.zeros((patches, 1), jnp.int32)
    at_row = lax.broadcasted_iota(jnp.int32, (1, patches), 1)
    at_col = lax.broadcasted_iota(jnp.int32, (patches, 1), 0)
    for image in range(len_ref.shape[1]):
        ends = ends + len_ref[:, image : image + 1]
        ids_row = ids_row + (at_row >= ends * 4).astype(jnp.int32)
        ids_col = ids_col + (at_col >= ends * 4).astype(jnp.int32)
    same = ids_col == ids_row
    for head in range(heads_wide // HD):
        query, keys, values = (
            qkv[c * heads_wide + head * HD : c * heads_wide + (head + 1) * HD].astype(kind) for c in range(3)
        )
        scores = lax.dot_general(keys, query, (((0,), (0,)), ((), ())), preferred_element_type=f32) * HD ** (-0.5)
        scores = jnp.where(same, scores, -1e30)
        top = jnp.max(scores, axis=0, keepdims=True)
        expo = jnp.exp(scores - top)
        weights = (expo / jnp.sum(expo, axis=0, keepdims=True)).astype(kind)
        att[head * HD : (head + 1) * HD] = jnp.dot(values, weights, preferred_element_type=f32).astype(kind)
    loads["wp"].wait()
    total = ScatterSum(part, buf["r1"], buf["yb"], buf["r2"], sem)
    for u in range(2):
        piece = lax.dot_general(
            att[...], buf["wp"][:, u * half : (u + 1) * half], (((0,), (0,)), ((), ())), preferred_element_type=f32
        )
        part[u] = piece.astype(kind).reshape(m, own, half)
        total.start(u)
    for u in range(2):
        total.forward(u)
    for u in range(2):
        at = slice(u * half, (u + 1) * half)
        vo[:, at] = vit_ref[:, at].astype(f32) + total.finish(u)
    second = normalize(vo[...], one_row(gain2_ref))
    for k in range(width // 128):
        buf["vs"][k] = second[:, k * 128 : (k + 1) * 128]
    tokens = own // 4

    def merged_view(u, at):
        return ag2.at[u - 2, :, at]

    gather_two = LineGather(merged_view, sem)
    for q in range(2):
        for j in range(4):
            for k in range(half // 128):
                ag2[q, j, mt, :, k * 128 : (k + 1) * 128] = buf["vs"][
                    q * half // 128 + k, pl.ds(j, tokens, stride=4), :
                ].astype(kind)
        gather_two.start(q + 2)
    for k in range(1, m_a):
        for u in range(2):
            gather_two.relay(u + 2, k)
    loads["w1"].wait()
    for u in range(2):
        gather_two.finish(u + 2)
    for piece, (start, stop) in enumerate(pieces_of(buf["w1"].shape[1])):
        expanded = None
        for u in range(2):
            for j in range(4):
                at = j * width + u * half
                term = jnp.dot(
                    ag2[u, j].reshape(m * tokens, half),
                    buf["w1"][at : at + half, start:stop],
                    preferred_element_type=f32,
                )
                expanded = term if expanded is None else expanded + term
        emit(piece, (0.5 * expanded * (1.0 + lax.erf(expanded * 0.5**0.5))).astype(kind))


def pieces_of(width):
    middle = -(-width // 256) * 128
    return [(0, middle), (middle, width)]


def vision_parts(own, width, heads_wide, hidden, kind):
    m, half, f32 = lax.axis_size("tp"), width // 2, jnp.float32
    shapes = {
        "ag": ((2, m, own, half), kind),
        "wq": ((3 * heads_wide, width), kind),
        "wp": ((heads_wide, width), kind),
        "w1": ((4 * width, hidden), kind),
        "qkv": ((3 * heads_wide, m * own), f32),
        "att": ((heads_wide, m * own), kind),
        "vo": ((own, width), f32),
        "vs": ((width // 128, own, 128), f32),
        "ag2": ((2, 4, m, own // 4, half), kind),
    }
    shapes |= scatter_shapes(2, 2, (own, half), kind)
    return shapes, {"wq": (), "wp": (), "w1": ()} | line_sems(4) | scatter_sems(2)


def step_kernel(
    parts, buf_names, sem_names, first_local, later_local, vit_ref, len_ref, vgain_ref, mgain_ref, pos_ref, gain_ref,
    wq_ref, wp_ref, w1_ref, w2_ref, w_ref, d_ref, out_ref, *scratch
):
    buf = dict(zip(buf_names, scratch))
    sem = dict(zip(sem_names, scratch[len(buf_names):]))
    n, m = lax.axis_size("seq"), lax.axis_size("tp")
    (n_a, n_b), (m_a, m_b) = factors(n), factors(m)
    me, mt = lax.axis_index("seq"), lax.axis_index("tp")
    a, b = me // n_b, lax.rem(me, n_b)
    ta, tb = mt // m_b, lax.rem(mt, m_b)
    x_peers, core_peers = grid_peers(n_a, n_b, a, b)
    t_major, t_minor = grid_peers(m_a, m_b, ta, tb)
    partner = core_peers[0]
    chunks, rows, depth = w_ref.shape[1:]
    steps = parts * chunks
    owned = steps // n_b
    count = n_a * 128
    block = count // m
    half = depth // 2
    tokens = parts * count
    places = one_row(pos_ref)

    def to(axis, src, dst, s, r, peer):
        return remote(src, dst, s, r, axis, peer)

    def lanes(owner):
        return pl.ds(pl.multiple_of(owner * 128, 128), 128)

    w2_load = pltpu.make_async_copy(
        w2_ref.at[:, pl.ds(pl.multiple_of(me * depth, depth), depth)], buf["w2s"], sem["w2"]
    )

    def w_load(i):
        slot = lax.rem(i, 2)
        return pltpu.make_async_copy(w_ref.at[:, lax.rem(i, chunks)], buf["held"].at[slot], sem["w"].at[slot])

    def d_load(i):
        slot = lax.rem(i, 2)
        return pltpu.make_async_copy(d_ref.at[lax.rem(i, chunks)], buf["dheld"].at[slot], sem["d"].at[slot])


    barrier = pltpu.get_barrier_semaphore()
    everyone = [("seq", lax.rem(me + d, n)) for d in range(1, n)]
    everyone += [("tp", peer) for peer in t_major + t_minor]

    def enter():
        pl.semaphore_wait(barrier, len(everyone))

    ex = buf["ex"]
    columns = [pl.ds(start, stop - start) for start, stop in pieces_of(ex.shape[2])]

    def ex_x(piece, da):
        own = ex.at[me, :, columns[piece]]
        return to("seq", own, own, sem["ea_s"].at[piece, da - 1], sem["ea_r"].at[piece, da - 1], x_peers[da - 1])

    def ex_core(piece, da):
        held = ex.at[lax.rem(a - da + n_a, n_a) * n_b + b, :, columns[piece]]
        return to("seq", held, held, sem["eb_s"].at[piece, da], sem["eb_r"].at[piece, da], partner)

    def emit(piece, values):
        ex[me, :, columns[piece]] = values
        for da in range(1, n_a):
            ex_x(piece, da).start()
        ex_core(piece, 0).start()

    def first_half(**own):
        loads = {
            k: pltpu.make_async_copy(ref, own["v_" + k], sem["v_" + k])
            for k, ref in (("wq", wq_ref), ("wp", wp_ref), ("w1", w1_ref))
        }
        for copy in loads.values():
            copy.start()
        w2_load.start()
        w_load(0).start()
        for axis, peer in everyone:
            pl.semaphore_signal(barrier, inc=1, device_id={axis: peer}, device_id_type=MESH)
        vision_stage(
            vit_ref, len_ref, vgain_ref, mgain_ref, loads, under("v_", buf | own), under("v_", sem), enter, emit
        )

    pl.run_scoped(first_half, **{k: pltpu.VMEM(*v) for k, v in first_local.items()})
    for piece in range(2):
        for da in range(1, n_a):
            ex_x(piece, da).wait_recv()
            ex_core(piece, da).start()
    for piece in range(2):
        for da in range(n_a):
            ex_core(piece, da).wait()
        for da in range(1, n_a):
            ex_x(piece, da).wait_send()

    def second_half(**own):
        buf.update(own)
        part, tok = buf["part"], buf["tok"]
        sums = ScatterSum(part, buf["r1"], buf["yb"], buf["r2"], sem)
        tokens_of = LineGather(lambda u, at: tok.at[u, at], sem)

        def ag_start(u):
            tok[u, mt] = sums.finish(u).astype(tok.dtype)
            tokens_of.start(u)

        rq, inv, sqa, nrm = buf["rq"], buf["inv"], buf["sqa"], buf["nrm"]

        def squares(h, d):
            return to(
                "seq", rq.at[h, me], rq.at[h, me], sem["q_s"].at[h, d - 1], sem["q_r"].at[h, d - 1], lax.rem(me + d, n)
            )

        def ag_finish(h):
            tokens_of.finish(h)
            first = lax.rem(h, 2) * half
            gain = one_row(gain_ref, lax.rem(h, 2) * (half // 128), half // 128)

            def rows_of(t, carry):
                values = tok[h, t].astype(jnp.float32)
                at = pl.ds(pl.multiple_of(t * block, block), block)
                cols = pl.ds(pl.multiple_of(first, 128), half)
                nrm[at, cols] = (values * gain).astype(nrm.dtype)
                total = values[:, :128] * values[:, :128]
                for k in range(1, half // 128):
                    piece = values[:, k * 128 : (k + 1) * 128]
                    total = total + piece * piece
                sqa[lax.rem(h, 2), at] = total
                return carry

            lax.fori_loop(0, m, rows_of, 0)

        def ag_both(h):
            ag_finish(2 * h)
            ag_finish(2 * h + 1)
            squared = jnp.sum(jnp.transpose(sqa[0] + sqa[1]), axis=0, keepdims=True)
            rq[h, me] = jnp.broadcast_to(squared, (8, count))
            for d in range(1, n):
                squares(h, d).start()

        def inverse(h):
            for d in range(1, n):
                squares(h, d).wait()
            total = rq[h, 0]
            for s in range(1, n):
                total = total + rq[h, s]
            inv[h] = lax.rsqrt(total / (depth * n) + 1e-06)

        w2_load.wait()
        for h in range(parts):
            row = lax.broadcasted_iota(jnp.int32, (count, tokens), 0)
            slot = lax.shift_right_logical(row, block.bit_length() - 1) * (block * (parts - 1)) + row + h * block
            pick = (slot == places).astype(jnp.bfloat16)
            moved = jnp.dot(
                pick, ex[...].reshape(tokens, ex.shape[2]), preferred_element_type=jnp.float32
            ).astype(jnp.bfloat16)
            width = min(512, half)
            for k in range(depth // width):
                piece = jnp.dot(
                    moved, buf["w2s"][:, k * width : (k + 1) * width], preferred_element_type=jnp.float32
                ).astype(part.dtype)
                q, at = k * width // half, k * width % half
                part[2 * h + q, :, :, at : at + width] = piece.reshape(m, block, width)
                if h == 0 and at + width == half:
                    sums.start(q)
        sums.forward(0)
        sums.forward(1)
        if parts > 1:
            sums.start(2)
        ag_start(0)
        ag_start(1)
        for k in range(1, m_a):
            for u in range(2):
                tokens_of.relay(u, k)
        if parts > 1:
            sums.start(3)
        ag_both(0)

        gu, pin, keep, yx, rx, hid, acc = (buf[k] for k in ("gu", "pin", "keep", "yx", "rx", "hid", "acc"))

        def owner(i):
            return lax.rem(i, n_b) == b

        def to_owner(i):
            return to("seq", gu.at[lax.rem(i, 2)], pin.at[i // n_b], sem["p_s"].at[i // n_b], sem["p_r"].at[i // n_b], partner)

        def to_x(i, da):
            o = i // n_b
            return to(
                "seq", yx.at[lax.rem(o, 4), da - 1], rx.at[o, da - 1], sem["y_s"].at[o, da - 1], sem["y_r"].at[o, da - 1], x_peers[da - 1]
            )

        def hid_x(i, da):
            target = hid.at[i, :, lanes(a)]
            return to("seq", target, target, sem["h_s"].at[i, da - 1], sem["h_r"].at[i, da - 1], x_peers[da - 1])

        def hid_core(i, da):
            target = hid.at[i, :, lanes(lax.rem(a - da + n_a, n_a))]
            return to("seq", target, target, sem["o_s"].at[i, da], sem["b_r"].at[i, da], partner)

        def stage_a(i):
            w_load(i).wait()

            @pl.when(i + 1 < steps)
            def _():
                w_load(i + 1).start()

            for half in range(2):
                gu[lax.rem(i, 2), half] = lax.dot_general(
                    buf["held"][lax.rem(i, 2), half],
                    nrm[...],
                    (((1,), (1,)), ((), ())),
                    preferred_element_type=jnp.float32,
                ).astype(gu.dtype)

            @pl.when(jnp.logical_not(owner(i)))
            def _():
                to_owner(i).start()

        def stage_b(i):
            o = i // n_b

            @pl.when(owner(i))
            def _():
                to_owner(i).wait_recv()

                def both(da):
                    at = lanes(lax.rem(a + da, n_a))
                    return gu[lax.rem(i, 2), :, :, at].astype(jnp.float32) + pin[o, :, :, at].astype(jnp.float32)

                for da in range(1, n_a):
                    yx[lax.rem(o, 4), da - 1] = both(da).astype(yx.dtype)
                    to_x(i, da).start()
                keep[lax.rem(o, 2)] = both(0)

            @pl.when(jnp.logical_not(owner(i)))
            def _():
                to_owner(i).wait_send()

        def stage_c(i):
            o, h = i // n_b, i // chunks

            @pl.when(lax.rem(i, chunks) == 0)
            def _():
                inverse(h)

            @pl.when(owner(i))
            def _():
                total = keep[lax.rem(o, 2)]
                for da in range(1, n_a):
                    to_x(i, da).wait()
                    total = total + rx[o, da - 1].astype(jnp.float32)
                total = total * inv[h, 0:1, lanes(a)]
                hid[i, :, lanes(a)] = (jax.nn.silu(total[0]) * total[1]).astype(hid.dtype)
                for da in range(1, n_a):
                    hid_x(i, da).start()
                hid_core(i, 0).start()

        def stage_d(i):
            @pl.when(owner(i))
            def _():
                for da in range(1, n_a):
                    hid_x(i, da).wait()
                    hid_core(i, da).start()

        def stage_e(i):
            c, h = lax.rem(i, chunks), i // chunks

            @pl.when(owner(i))
            def _():
                for da in range(n_a):
                    hid_core(i, da).wait_send()

            @pl.when(jnp.logical_not(owner(i)))
            def _():
                for da in range(n_a):
                    hid_core(i, da).wait_recv()

            d_load(i).wait()
            width = min(512, depth)
            left = hid[i]
            for k in range(depth // width):
                at = slice(k * width, (k + 1) * width)
                piece = lax.dot_general(
                    left, buf["dheld"][lax.rem(i, 2), :, at], (((0,), (0,)), ((), ())), preferred_element_type=jnp.float32
                )

                @pl.when(c == 0)
                def _():
                    acc[:, at] = piece

                @pl.when(c > 0)
                def _():
                    acc[:, at] += piece

            @pl.when(c == chunks - 1)
            def _():
                for q in range(2):
                    u = 2 * parts + 2 * h + q
                    part[2 * h + q] = acc[:, q * half : (q + 1) * half].astype(part.dtype).reshape(m, block, half)
                    sums.start(u)

        def down_pass(h):
            sums.forward(2 * parts + 2 * h)
            sums.forward(2 * parts + 2 * h + 1)

        def output(h):
            at = pl.ds(pl.multiple_of(h * block, block), block)
            for q in range(2):
                total = sums.finish(2 * parts + 2 * h + q)
                out_ref[at, q * half : (q + 1) * half] = (
                    tok[2 * h + q, mt].astype(jnp.float32) + total
                ).astype(out_ref.dtype)

        def iteration(i, carry):
            def when(lag, fn):
                @pl.when(jnp.logical_and(i >= lag, i - lag < steps))
                def _():
                    fn(i - lag)

            h, k = i // chunks, lax.rem(i, chunks)
            more = h + 1 < parts

            def at_step(step, q, fn):
                @pl.when(jnp.logical_and(more, k == step * chunks // 7))
                def _():
                    fn(2 * h + 2 + q)

            @pl.when(jnp.logical_and(jnp.logical_and(i > 0, i < steps), k == 0))
            def _():
                @pl.when(more)
                def _():
                    sums.start(2 * h + 2)
                    sums.start(2 * h + 3)

                ag_both(h)

            when(LAG_E - 1, lambda j: d_load(j).start())
            when(0, stage_a)
            when(1, stage_b)
            when(LAG_C, stage_c)
            when(LAG_D, stage_d)
            for q in range(2):
                at_step(AT_PASS[q], q, sums.forward)
            for q in range(2):
                at_step(AT_GATHER[q], q, ag_start)
            for hop in range(1, m_a):
                for q in range(2):
                    at_step(AT_RELAY[q] + hop, q, lambda u, hop=hop: tokens_of.relay(u, hop))
            when(LAG_E, stage_e)

            def later(lag, fn):
                @pl.when(jnp.logical_and(i - lag >= chunks, jnp.logical_and(lax.rem(i - lag + chunks, chunks) == 0, i - lag < steps)))
                def _():
                    fn((i - lag) // chunks - 1)

            later(LAG_E + 1, down_pass)
            later(LAG_E + 3, output)
            return carry

        lax.fori_loop(0, steps + LAG_E, iteration, 0)
        down_pass(parts - 1)
        output(parts - 1)

    pl.run_scoped(second_half, **{k: pltpu.VMEM(*v) for k, v in later_local.items()})


def whole_step(vit, lengths, vgain, mgain, positions, gain, w_qkv, w_proj, w1, w2, weight, down):
    n, m = lax.axis_size("seq"), lax.axis_size("tp")
    (n_a, n_b), (m_a, m_b) = factors(n), factors(m)
    _, chunks, rows, depth = weight.shape
    tokens = positions.size
    count = n_a * 128
    parts = tokens // count
    steps = parts * chunks
    block = count // m
    assert n_b == 2 and steps % 2 == 0 and chunks >= 7
    kind, f32 = vit.dtype, jnp.float32
    own, width = vit.shape
    group = m * own // 4
    shapes = {
        "ex": ((n, group, w1.shape[1]), kind),
        "w2s": ((w2.shape[0], depth), kind),
        "tok": ((2 * parts, m, block, depth // 2), kind),
        "nrm": ((count, depth), kind),
        "sqa": ((2, count, 128), f32),
        "rq": ((parts, n, 8, count), f32),
        "inv": ((parts, 8, count), f32),
        "held": ((2, 2, rows, depth), kind),
        "dheld": ((2, rows, depth), kind),
        "gu": ((2, 2, rows, count), kind),
        "pin": ((steps // 2, 2, rows, count), kind),
        "keep": ((2, 2, rows, 128), f32),
        "yx": ((4, n_a - 1, 2, rows, 128), kind),
        "rx": ((steps // 2, n_a - 1, 2, rows, 128), kind),
        "hid": ((steps, rows, count), kind),
        "acc": ((count, depth), f32),
    }
    shapes |= scatter_shapes(4 * parts, 2 * parts, (block, depth // 2), kind)
    sems = {
        "w2": (),
        "w": (2,),
        "d": (2,),
        "ea_s": (2, n_a),
        "ea_r": (2, n_a),
        "eb_s": (2, n_a),
        "eb_r": (2, n_a),
        "q_s": (parts, n),
        "q_r": (parts, n),
        "p_s": (steps // 2,),
        "p_r": (steps // 2,),
        "y_s": (steps // 2, n_a),
        "y_r": (steps // 2, n_a),
        "h_s": (steps, n_a),
        "h_r": (steps, n_a),
        "o_s": (steps, n_a),
        "b_r": (steps, n_a),
    }
    sems |= scatter_sems(4 * parts) | line_sems(2 * parts)
    v_shapes, v_sems = vision_parts(own, width, w_proj.shape[0], w1.shape[1], kind)
    shapes |= keyed("v_", v_shapes)
    sems |= keyed("v_", v_sems)
    first = ("v_wq", "v_wp", "v_w1", "v_qkv", "v_att", "v_vo", "v_vs", "v_part", "v_yb")
    first_local = {k: shapes.pop(k) for k in first}
    later = ("dheld", "acc", "keep", "yx", "gu", "nrm", "sqa", "part", "yb")
    later_local = {k: shapes.pop(k) for k in later}
    anywhere = pl.BlockSpec(memory_space=pl.ANY)
    return pl.pallas_call(
        functools.partial(step_kernel, parts, tuple(shapes), tuple(sems), first_local, later_local),
        out_shape=jax.ShapeDtypeStruct((tokens // m, depth), kind),
        in_specs=[VM] * 6 + [anywhere] * 6,
        out_specs=VM,
        scratch_shapes=[pltpu.VMEM(*v) for v in shapes.values()]
        + [pltpu.SemaphoreType.DMA(v) if v else pltpu.SemaphoreType.DMA for v in sems.values()],
        name="step",
        compiler_params=pltpu.CompilerParams(
            collective_id=0, has_side_effects=True, vmem_limit_bytes=67_000_000
        ),
    )(vit, lengths, vgain, mgain, positions, gain, w_qkv, w_proj, w1, w2, weight, down)


def chunk_count(rows):
    for count in (7, 6, 4, 3, 2):
        if rows % (count * 8) == 0:
            return count
    return 1


def local(
    vit_input,
    image_lengths,
    positions,
    vit_ln_gain,
    w_qkv,
    w_proj,
    merger_ln_gain,
    merger_w1,
    merger_w2,
    norm_gain,
    gate_up_weight,
    down_weight,
):
    width, _, head_cols = w_qkv.shape
    slice_width = norm_gain.shape[0]
    hidden_width = gate_up_weight.shape[2]
    chunks = chunk_count(hidden_width)
    rows = hidden_width // chunks
    return whole_step(
        vit_input,
        image_lengths,
        lane_rows(vit_ln_gain),
        lane_rows(merger_ln_gain),
        lane_rows(positions),
        lane_rows(norm_gain),
        w_qkv.transpose(1, 2, 0).reshape(3 * head_cols, width),
        w_proj,
        merger_w1,
        merger_w2,
        gate_up_weight.transpose(1, 2, 0).reshape(2, chunks, rows, slice_width),
        down_weight.reshape(chunks, rows, slice_width),
    )


def solution(mesh):
    return jax.shard_map(
        local,
        mesh=mesh,
        in_specs=(
            P(("seq", "tp"), None),
            P("seq", None),
            P(),
            P(),
            P(None, None, "tp"),
            P("tp", None),
            P(),
            P(None, "tp"),
            P("tp", None),
            P("seq"),
            P("seq", None, "tp"),
            P("tp", "seq"),
        ),
        out_specs=P("tp", "seq"),
        check_vma=False,
    )
```

time: 206 us -> 201 us (0.976)
  Pallas kernels: 202 us -> 199 us
  local copies, waits for them, and re-layouts: 4.26 us -> 1.67 us
    pallas_call x2 -> x1, Pallas kernels: 202 us -> 199 us  [whole_step(): pl.pallas_call(functools.partial(step_kernel, parts, tuple(shapes), tuple...]
    broadcast_in_dim x2 -> x0, local copies, waits for them, and re-layouts: 2.59 us -> none  [the longest x1 1.29 us: local(): merger_ln_gain[None, :]]
where the time goes in v3:
time: 201 us; the launch traced here: 200 us
  Pallas kernels  199 us (99%)
    pallas_call x1, Pallas kernels, whole_step(): pl.pallas_call(functools.partial(step_kernel, parts, tuple(shapes), tuple...  199 us

profile of v3, /device:TPU:0, one launch (start us, length us, event | category | flops | bytes accessed | tf_op | source)
XLA Modules:
  0.0 200.5 jit_solution(12497493777205489054)
XLA Ops:
  0.0 198.8 %step.1 = bf16[64,2048]{1,0:T(8,128)(2,1)} custom-call(bf16[64,1280]{1,0:T(8,128)(2,1)} %vit_ref.1, s32[1,2]{1,0:T(1,128)} %len_ref.1, f32[10,128]{1,0:T(8,128)} %bitcast.14, f32[10,128]{1,0:T(8,128)} %bitcast.15, s32[4,128]{1,0:T(4,128)} %bitcast.17, f32[16,128]{1,0:T(8,128)} %bitcast.16, bf16[480,1280]{1,0:T(8,128)(2,1)} %bitcast.13, ...), custom_call_target="tpu_custom_call" | custom-call | tf_op jit(solution)/shard_map/step/pallas_call | solution.py:754
  198.8 1.7 copy.14

commit v4 on v3

--- a/solution.py
+++ b/solution.py
@@ -10,6 +10,7 @@
 HD = 80
 MESH = pl.DeviceIdType.MESH
 LAG_C, LAG_D, LAG_E = 3, 5, 6
+UNITS = 2
 AT_PASS, AT_GATHER, AT_RELAY = (0, 1), (2, 3), (2, 3)
 VM = pl.BlockSpec(memory_space=pltpu.VMEM)
 
@@ -204,12 +205,13 @@
     m_a, m_b = factors(m)
     mt = lax.axis_index("tp")
     own, width = vit_ref.shape
-    half = width // 2
+    half = buf["ag"].shape[-1]
+    units = width // half
     heads_wide = buf["wp"].shape[0]
     f32, kind = jnp.float32, vit_ref.dtype
     ag, ag2, vo, part, qkv, att = (buf[k] for k in ("ag", "ag2", "vo", "part", "qkv", "att"))
     first = normalize(vit_ref[...].astype(f32), one_row(gain_ref)).astype(kind)
-    for q in range(2):
+    for q in range(units):
         ag[q, mt] = first[:, q * half : (q + 1) * half]
     enter()
 
@@ -217,14 +219,14 @@
         return ag.at[u, at]
 
     gather_one = LineGather(unit_view, sem)
-    for u in range(2):
+    for u in range(units):
         gather_one.start(u)
     for k in range(1, m_a):
-        for u in range(2):
+        for u in range(units):
             gather_one.relay(u, k)
     loads["wq"].wait()
     patches = m * own
-    for u in range(2):
+    for u in range(units):
         gather_one.finish(u)
         piece = lax.dot_general(
             buf["wq"][:, u * half : (u + 1) * half],
@@ -259,15 +261,15 @@
         att[head * HD : (head + 1) * HD] = jnp.dot(values, weights, preferred_element_type=f32).astype(kind)
     loads["wp"].wait()
     total = ScatterSum(part, buf["r1"], buf["yb"], buf["r2"], sem)
-    for u in range(2):
+    for u in range(units):
         piece = lax.dot_general(
             att[...], buf["wp"][:, u * half : (u + 1) * half], (((0,), (0,)), ((), ())), preferred_element_type=f32
         )
         part[u] = piece.astype(kind).reshape(m, own, half)
         total.start(u)
-    for u in range(2):
+    for u in range(units):
         total.forward(u)
-    for u in range(2):
+    for u in range(units):
         at = slice(u * half, (u + 1) * half)
         vo[:, at] = vit_ref[:, at].astype(f32) + total.finish(u)
     second = normalize(vo[...], one_row(gain2_ref))
@@ -276,33 +278,41 @@
     tokens = own // 4
 
     def merged_view(u, at):
-        return ag2.at[u - 2, :, at]
+        return ag2.at[u - units, :, at]
 
     gather_two = LineGather(merged_view, sem)
-    for q in range(2):
+    for q in range(units):
         for j in range(4):
             for k in range(half // 128):
                 ag2[q, j, mt, :, k * 128 : (k + 1) * 128] = buf["vs"][
                     q * half // 128 + k, pl.ds(j, tokens, stride=4), :
                 ].astype(kind)
-        gather_two.start(q + 2)
+        gather_two.start(q + units)
     for k in range(1, m_a):
-        for u in range(2):
-            gather_two.relay(u + 2, k)
+        for u in range(units):
+            gather_two.relay(u + units, k)
     loads["w1"].wait()
-    for u in range(2):
-        gather_two.finish(u + 2)
-    for piece, (start, stop) in enumerate(pieces_of(buf["w1"].shape[1])):
-        expanded = None
-        for u in range(2):
-            for j in range(4):
-                at = j * width + u * half
-                term = jnp.dot(
-                    ag2[u, j].reshape(m * tokens, half),
-                    buf["w1"][at : at + half, start:stop],
-                    preferred_element_type=f32,
-                )
-                expanded = term if expanded is None else expanded + term
+    pieces = pieces_of(buf["w1"].shape[1])
+
+    def product(u, piece):
+        start, stop = pieces[piece]
+        total = None
+        for j in range(4):
+            at = j * width + u * half
+            term = jnp.dot(
+                ag2[u, j].reshape(m * tokens, half), buf["w1"][at : at + half, start:stop], preferred_element_type=f32
+            )
+            total = term if total is None else total + term
+        return total
+
+    sums = [0.0, 0.0]
+    for u in range(units - 1):
+        gather_two.finish(u + units)
+        for piece in range(2):
+            sums[piece] = sums[piece] + product(u, piece)
+    gather_two.finish(2 * units - 1)
+    for piece in range(2):
+        expanded = sums[piece] + product(units - 1, piece)
         emit(piece, (0.5 * expanded * (1.0 + lax.erf(expanded * 0.5**0.5))).astype(kind))
 
 
@@ -313,8 +323,9 @@
 
 def vision_parts(own, width, heads_wide, hidden, kind):
     m, half, f32 = lax.axis_size("tp"), width // 2, jnp.float32
+    units = width // half
     shapes = {
-        "ag": ((2, m, own, half), kind),
+        "ag": ((units, m, own, half), kind),
         "wq": ((3 * heads_wide, width), kind),
         "wp": ((heads_wide, width), kind),
         "w1": ((4 * width, hidden), kind),
@@ -322,10 +333,10 @@
         "att": ((heads_wide, m * own), kind),
         "vo": ((own, width), f32),
         "vs": ((width // 128, own, 128), f32),
-        "ag2": ((2, 4, m, own // 4, half), kind),
+        "ag2": ((units, 4, m, own // 4, half), kind),
     }
-    shapes |= scatter_shapes(2, 2, (own, half), kind)
-    return shapes, {"wq": (), "wp": (), "w1": ()} | line_sems(4) | scatter_sems(2)
+    shapes |= scatter_shapes(units, units, (own, half), kind)
+    return shapes, {"wq": (), "wp": (), "w1": ()} | line_sems(2 * units) | scatter_sems(units)
 
 
 def step_kernel(
@@ -347,7 +358,7 @@
     owned = steps // n_b
     count = n_a * 128
     block = count // m
-    half = depth // 2
+    half = depth // UNITS
     tokens = parts * count
     places = one_row(pos_ref)
 
@@ -439,8 +450,8 @@
 
         def ag_finish(h):
             tokens_of.finish(h)
-            first = lax.rem(h, 2) * half
-            gain = one_row(gain_ref, lax.rem(h, 2) * (half // 128), half // 128)
+            first = lax.rem(h, UNITS) * half
+            gain = one_row(gain_ref, lax.rem(h, UNITS) * (half // 128), half // 128)
 
             def rows_of(t, carry):
                 values = tok[h, t].astype(jnp.float32)
@@ -451,15 +462,15 @@
                 for k in range(1, half // 128):
                     piece = values[:, k * 128 : (k + 1) * 128]
                     total = total + piece * piece
-                sqa[lax.rem(h, 2), at] = total
+                sqa[lax.rem(h, UNITS), at] = total
                 return carry
 
             lax.fori_loop(0, m, rows_of, 0)
 
         def ag_both(h):
-            ag_finish(2 * h)
-            ag_finish(2 * h + 1)
-            squared = jnp.sum(jnp.transpose(sqa[0] + sqa[1]), axis=0, keepdims=True)
+            for q in range(UNITS):
+                ag_finish(UNITS * h + q)
+            squared = jnp.sum(jnp.transpose(jnp.sum(sqa[...], axis=0)), axis=0, keepdims=True)
             rq[h, me] = jnp.broadcast_to(squared, (8, count))
             for d in range(1, n):
                 squares(h, d).start()
@@ -486,20 +497,20 @@
                     moved, buf["w2s"][:, k * width : (k + 1) * width], preferred_element_type=jnp.float32
                 ).astype(part.dtype)
                 q, at = k * width // half, k * width % half
-                part[2 * h + q, :, :, at : at + width] = piece.reshape(m, block, width)
+                part[UNITS * h + q, :, :, at : at + width] = piece.reshape(m, block, width)
                 if h == 0 and at + width == half:
                     sums.start(q)
-        sums.forward(0)
-        sums.forward(1)
+        for u in range(UNITS):
+            sums.forward(u)
+        for t in range(UNITS + m_a - 1):
+            if t < UNITS:
+                ag_start(t)
+            for k in range(1, m_a):
+                if 0 <= t - k < UNITS:
+                    tokens_of.relay(t - k, k)
         if parts > 1:
-            sums.start(2)
-        ag_start(0)
-        ag_start(1)
-        for k in range(1, m_a):
-            for u in range(2):
-                tokens_of.relay(u, k)
-        if parts > 1:
-            sums.start(3)
+            for u in range(UNITS, 2 * UNITS):
+                sums.start(u)
         ag_both(0)
 
         gu, pin, keep, yx, rx, hid, acc = (buf[k] for k in ("gu", "pin", "keep", "yx", "rx", "hid", "acc"))
@@ -603,7 +614,7 @@
                     hid_core(i, da).wait_recv()
 
             d_load(i).wait()
-            width = min(512, depth)
+            width = min(512, half)
             left = hid[i]
             for k in range(depth // width):
                 at = slice(k * width, (k + 1) * width)
@@ -615,27 +626,28 @@
                 def _():
                     acc[:, at] = piece
 
-                @pl.when(c > 0)
+                @pl.when(jnp.logical_and(c > 0, c < chunks - 1))
                 def _():
                     acc[:, at] += piece
 
-            @pl.when(c == chunks - 1)
-            def _():
-                for q in range(2):
-                    u = 2 * parts + 2 * h + q
-                    part[2 * h + q] = acc[:, q * half : (q + 1) * half].astype(part.dtype).reshape(m, block, half)
-                    sums.start(u)
+                @pl.when(c == chunks - 1)
+                def _():
+                    q, first = k * width // half, k * width % half
+                    last = (acc[:, at] + piece).astype(part.dtype)
+                    part[UNITS * h + q, :, :, first : first + width] = last.reshape(m, block, width)
+                    if first + width == half:
+                        sums.start((parts + h) * UNITS + q)
 
         def down_pass(h):
-            sums.forward(2 * parts + 2 * h)
-            sums.forward(2 * parts + 2 * h + 1)
+            for q in range(UNITS):
+                sums.forward((parts + h) * UNITS + q)
 
         def output(h):
             at = pl.ds(pl.multiple_of(h * block, block), block)
-            for q in range(2):
-                total = sums.finish(2 * parts + 2 * h + q)
+            for q in range(UNITS):
+                total = sums.finish((parts + h) * UNITS + q)
                 out_ref[at, q * half : (q + 1) * half] = (
-                    tok[2 * h + q, mt].astype(jnp.float32) + total
+                    tok[UNITS * h + q, mt].astype(jnp.float32) + total
                 ).astype(out_ref.dtype)
 
         def iteration(i, carry):
@@ -650,14 +662,14 @@
             def at_step(step, q, fn):
                 @pl.when(jnp.logical_and(more, k == step * chunks // 7))
                 def _():
-                    fn(2 * h + 2 + q)
+                    fn(UNITS * (h + 1) + q)
 
             @pl.when(jnp.logical_and(jnp.logical_and(i > 0, i < steps), k == 0))
             def _():
                 @pl.when(more)
                 def _():
-                    sums.start(2 * h + 2)
-                    sums.start(2 * h + 3)
+                    for q in range(UNITS):
+                        sums.start(UNITS * (h + 1) + q)
 
                 ag_both(h)
 
@@ -666,13 +678,13 @@
             when(1, stage_b)
             when(LAG_C, stage_c)
             when(LAG_D, stage_d)
-            for q in range(2):
-                at_step(AT_PASS[q], q, sums.forward)
-            for q in range(2):
-                at_step(AT_GATHER[q], q, ag_start)
+            for q in range(UNITS):
+                at_step(AT_PASS[q * 2 // UNITS], q, sums.forward)
+            for q in range(UNITS):
+                at_step(AT_GATHER[q * 2 // UNITS], q, ag_start)
             for hop in range(1, m_a):
-                for q in range(2):
-                    at_step(AT_RELAY[q] + hop, q, lambda u, hop=hop: tokens_of.relay(u, hop))
+                for q in range(UNITS):
+                    at_step(AT_RELAY[q * 2 // UNITS] + hop, q, lambda u, hop=hop: tokens_of.relay(u, hop))
             when(LAG_E, stage_e)
 
             def later(lag, fn):
@@ -707,9 +719,9 @@
     shapes = {
         "ex": ((n, group, w1.shape[1]), kind),
         "w2s": ((w2.shape[0], depth), kind),
-        "tok": ((2 * parts, m, block, depth // 2), kind),
+        "tok": ((UNITS * parts, m, block, depth // UNITS), kind),
         "nrm": ((count, depth), kind),
-        "sqa": ((2, count, 128), f32),
+        "sqa": ((UNITS, count, 128), f32),
         "rq": ((parts, n, 8, count), f32),
         "inv": ((parts, 8, count), f32),
         "held": ((2, 2, rows, depth), kind),
@@ -722,7 +734,7 @@
         "hid": ((steps, rows, count), kind),
         "acc": ((count, depth), f32),
     }
-    shapes |= scatter_shapes(4 * parts, 2 * parts, (block, depth // 2), kind)
+    shapes |= scatter_shapes(2 * UNITS * parts, UNITS * parts, (block, depth // UNITS), kind)
     sems = {
         "w2": (),
         "w": (2,),
@@ -742,7 +754,7 @@
         "o_s": (steps, n_a),
         "b_r": (steps, n_a),
     }
-    sems |= scatter_sems(4 * parts) | line_sems(2 * parts)
+    sems |= scatter_sems(2 * UNITS * parts) | line_sems(UNITS * parts)
     v_shapes, v_sems = vision_parts(own, width, w_proj.shape[0], w1.shape[1], kind)
     shapes |= keyed("v_", v_shapes)
     sems |= keyed("v_", v_sems)

time: 201 us -> 197 us (0.980)
  Pallas kernels: 199 us -> 195 us
    pallas_call x1, Pallas kernels: 199 us -> 195 us  [whole_step(): pl.pallas_call(functools.partial(step_kernel, parts, tuple(shapes), tuple...]
where the time goes in v4:
time: 197 us
  Pallas kernels  195 us (99%)
    pallas_call x1, Pallas kernels, whole_step(): pl.pallas_call(functools.partial(step_kernel, parts, tuple(shapes), tuple...  195 us

profile of v4, /device:TPU:0, one launch (start us, length us, event | category | flops | bytes accessed | tf_op | source)
XLA Modules:
  0.0 196.8 jit_solution(12230129890970526674)
XLA Ops:
  0.0 195.1 %step.1 = bf16[64,2048]{1,0:T(8,128)(2,1)} custom-call(bf16[64,1280]{1,0:T(8,128)(2,1)} %vit_ref.1, s32[1,2]{1,0:T(1,128)} %len_ref.1, f32[10,128]{1,0:T(8,128)} %bitcast.14, f32[10,128]{1,0:T(8,128)} %bitcast.15, s32[4,128]{1,0:T(4,128)} %bitcast.17, f32[16,128]{1,0:T(8,128)} %bitcast.16, bf16[480,1280]{1,0:T(8,128)(2,1)} %bitcast.13, ...), custom_call_target="tpu_custom_call" | custom-call | tf_op jit(solution)/shard_map/step/pallas_call | solution.py:766
  195.1 1.7 copy.14
